TPU v7x, 32 devices: a whole 2x2x4 slice. The times are simulated.
32 devices in a mesh: shard: 4 (over y, x), ctx: 2 (over core), tp: 4 (over z).
Axes of the slice: x: 2, y: 2, z: 4, core: 2. Of those that a mesh axis runs over, the one named last changes fastest.
Arguments:
- hidden_in: bfloat16 [4, 4, 512, 2048], P('shard', 'ctx'), may hold values from -6 to 6
- grad_out: bfloat16 [4, 4, 512, 2048], P('shard', 'ctx'), may hold values from -6 to 6
- segment_ids: int32 [4, 2048], P('shard'), may hold values from 0 to 5, never falling along the last dimension, each value on 1 to 1024 neighbouring positions
- group_order: int32 [4], replicated, may hold values from 0 to 3, each once
- ln1_gain: bfloat16 [2048], P('shard'), may hold values from 0.5 to 1.5
- ln1_bias: bfloat16 [2048], P('shard'), may hold values from -3 to 3
- qkv_weight: bfloat16 [2048, 6144], P('shard', 'tp'), may hold values from -3 to 3
- qkv_bias: bfloat16 [4, 1536], P('tp', 'shard'), may hold values from -3 to 3
- dense_weight: bfloat16 [2048, 2048], P('shard', 'tp'), may hold values from -0.375 to 0.375
- dense_bias: bfloat16 [2048], P('shard'), may hold values from -3 to 3
- ln2_gain: bfloat16 [2048], P('shard'), may hold values from 0.5 to 1.5
- ln2_bias: bfloat16 [2048], P('shard'), may hold values from -3 to 3
- up_weight: bfloat16 [2048, 8192], P('shard', 'tp'), may hold values from -0.125 to 0.125
- up_bias: bfloat16 [4, 2048], P('tp', 'shard'), may hold values from -3 to 3
- down_weight: bfloat16 [2048, 8192], P('shard', 'tp'), may hold values from -0.0625 to 0.0625
- down_bias: bfloat16 [2048], P('shard'), may hold values from -3 to 3
Outputs:
- output: float32 [4, 4, 512, 2048], P('shard', 'ctx', None, 'tp')
- input_grad: float32 [4, 4, 512, 2048], P('shard', 'ctx', None, 'tp')
- ln1_gain_grad: float32 [2048], P('shard')
- ln1_bias_grad: float32 [2048], P('shard')
- qkv_weight_grad: float32 [2048, 6144], P('shard', 'tp')
- qkv_bias_grad: float32 [4, 1536], P('tp', 'shard')
- dense_weight_grad: float32 [2048, 2048], P('shard', 'tp')
- out_bias_grad: float32 [2048], P('shard')
- ln2_gain_grad: float32 [2048], P('shard')
- ln2_bias_grad: float32 [2048], P('shard')
- up_weight_grad: float32 [2048, 8192], P('shard', 'tp')
- up_bias_grad: float32 [4, 2048], P('tp', 'shard')
- down_weight_grad: float32 [2048, 8192], P('shard', 'tp')
Inputs may be any that keep to these rules, and one draw needn't show every extreme that they name: A permutation: stored block k of every row holds the row's places group_order[k] * 512 to group_order[k] * 512 + 511. `segment_ids`: never falling along a row; each segment has 1 to 1024 tokens, one exactly 1024.
All inputs are finite; a program needn't handle non-finite values.
Results may differ from a plain program's by a relative error of at most 0.012.
Values may be sent and summed in bfloat16 or wider, within the bound.
A program may use at most 320 MiB of HBM per device.

v0:
```python
import functools
import math

import jax
import jax.numpy as jnp
from jax import lax
from jax.experimental import pallas as pl
from jax.experimental.pallas import tpu as pltpu
from jax.sharding import PartitionSpec as P


HD = 256
ROT = 64
LANES = 128

EPSILON = 1e-05
ROTARY_BASE = 10000.0
NEG = -1e30
VMEM_LIMIT = 56 * 1024 * 1024


def segment_positions(segments):
    length_all = segments.shape[0]
    index_row = jnp.arange(length_all, dtype=jnp.int32)
    changed = jnp.concatenate(
        [jnp.ones((1,), dtype=jnp.bool_), segments[1:] != segments[:-1]]
    )
    seg_start = jnp.where(changed, index_row, jnp.zeros_like(segments))
    return index_row - lax.cummax(seg_start, axis=0)


def rotary_tables(positions):
    half_rot = ROT // 2
    frequency = ROTARY_BASE ** (-2.0 * jnp.arange(half_rot, dtype=jnp.float32) / ROT)
    angles = positions.astype(jnp.float32)[:, None] * frequency[None, :]
    cosine, sine = jnp.cos(angles), jnp.sin(angles)
    count = positions.shape[0]
    rest_one = jnp.ones((count, LANES - ROT), jnp.float32)
    rest_zero = jnp.zeros((count, LANES - half_rot), jnp.float32)
    cosine_table = jnp.concatenate([cosine, cosine, rest_one], axis=1)
    low_table = jnp.concatenate([-sine, rest_zero], axis=1)
    high_table = jnp.concatenate(
        [jnp.zeros_like(sine), sine, rest_zero[:, : LANES - ROT]], axis=1
    )
    return cosine_table, low_table, high_table


def turn(values, cosine, low, high, sign):
    half_rot = ROT // 2
    down = pltpu.roll(values, LANES - half_rot, 1)
    up = pltpu.roll(values, half_rot, 1)
    return values * cosine + sign * (down * low + up * high)


def contract_first(left_mat, right_mat):
    return lax.dot_general(
        left_mat, right_mat, (((0,), (0,)), ((), ())), preferred_element_type=jnp.float32
    )


def contract_last(left_mat, right_mat):
    return lax.dot_general(
        left_mat, right_mat, (((1,), (1,)), ((), ())), preferred_element_type=jnp.float32
    )


def block_meets(bounds_ref, order_ref, q_index, k_index):
    return (
        (order_ref[k_index] <= order_ref[q_index])
        & (bounds_ref[0, k_index] <= bounds_ref[1, q_index])
        & (bounds_ref[1, k_index] >= bounds_ref[0, q_index])
    )


def pair_mask(order_ref, seg_col_ref, seg_row_ref, q_index, k_index, block):
    q_place = order_ref[q_index] * block + lax.broadcasted_iota(jnp.int32, (block, block), 0)
    k_place = order_ref[k_index] * block + lax.broadcasted_iota(jnp.int32, (block, block), 1)
    seg_q = seg_col_ref[pl.ds(q_index * block, block), :]
    seg_k = seg_row_ref[:, pl.ds(pl.multiple_of(k_index * block, block), block)]
    return (k_place <= q_place) & (seg_q == seg_k)


def attend_kernel(
    order_ref,
    bounds_ref,
    proj_ref,
    cos_ref,
    low_ref,
    high_ref,
    seg_col_ref,
    seg_row_ref,
    query_ref,
    key_ref,
    value_ref,
    attn_ref,
    lse_ref,
    top_ref,
    sum_ref,
    acc_ref,
    *,
    block,
    count,
):
    score_scale = 1.0 / math.sqrt(HD)
    for index in range(count):
        rows = pl.ds(index * block, block)
        tables = (cos_ref[rows, :], low_ref[rows, :], high_ref[rows, :])
        for start, out in ((0, query_ref), (HD, key_ref)):
            out[rows, :LANES] = turn(
                proj_ref[rows, start : start + LANES], *tables, 1.0
            ).astype(jnp.bfloat16)
            out[rows, LANES:] = proj_ref[rows, start + LANES : start + HD].astype(jnp.bfloat16)
        value_ref[rows, :] = proj_ref[rows, 2 * HD :].astype(jnp.bfloat16)

    @pl.loop(0, count)
    def _(q_index):
        rows = pl.ds(pl.multiple_of(q_index * block, block), block)
        top_ref[...] = jnp.full_like(top_ref, NEG)
        sum_ref[...] = jnp.zeros_like(sum_ref)
        acc_ref[...] = jnp.zeros_like(acc_ref)

        @pl.loop(0, count)
        def _(k_index):
            @pl.when(block_meets(bounds_ref, order_ref, q_index, k_index))
            def _():
                keys = pl.ds(pl.multiple_of(k_index * block, block), block)
                scores = contract_last(query_ref[rows, :], key_ref[keys, :]) * score_scale
                allowed = pair_mask(order_ref, seg_col_ref, seg_row_ref, q_index, k_index, block)
                scores = jnp.where(allowed, scores, NEG)
                old_top = top_ref[...]
                new_top = jnp.maximum(old_top, jnp.max(scores, axis=1, keepdims=True))
                shrink = jnp.exp(old_top - new_top)
                weights = jnp.where(allowed, jnp.exp(scores - new_top), 0.0)
                top_ref[...] = new_top
                sum_ref[...] = sum_ref[...] * shrink + jnp.sum(weights, axis=1, keepdims=True)
                acc_ref[...] = acc_ref[...] * shrink + jnp.dot(
                    weights.astype(jnp.bfloat16),
                    value_ref[keys, :],
                    preferred_element_type=jnp.float32,
                )

        attn_ref[rows, :] = (acc_ref[...] / sum_ref[...]).astype(jnp.bfloat16)
        lse_ref[rows, :] = top_ref[...] + jnp.log(sum_ref[...])


def attend_grad_kernel(
    order_ref,
    bounds_ref,
    query_ref,
    key_ref,
    value_ref,
    attn_ref,
    grad_ref,
    lse_ref,
    cos_ref,
    low_ref,
    high_ref,
    seg_col_ref,
    seg_row_ref,
    out_ref,
    sums_ref,
    query_acc,
    key_acc,
    value_acc,
    delta_ref,
    *,
    block,
    count,
):
    score_scale = 1.0 / math.sqrt(HD)
    query_acc[...] = jnp.zeros_like(query_acc)
    delta_ref[...] = jnp.sum(
        grad_ref[...].astype(jnp.float32) * attn_ref[...].astype(jnp.float32),
        axis=1,
        keepdims=True,
    )

    @pl.loop(0, count)
    def _(k_index):
        keys = pl.ds(pl.multiple_of(k_index * block, block), block)
        key_acc[...] = jnp.zeros_like(key_acc)
        value_acc[...] = jnp.zeros_like(value_acc)

        @pl.loop(0, count)
        def _(q_index):
            @pl.when(block_meets(bounds_ref, order_ref, q_index, k_index))
            def _():
                rows = pl.ds(pl.multiple_of(q_index * block, block), block)
                query, key_rows = query_ref[rows, :], key_ref[keys, :]
                grad_rows = grad_ref[rows, :]
                scores = contract_last(query, key_rows) * score_scale
                allowed = pair_mask(order_ref, seg_col_ref, seg_row_ref, q_index, k_index, block)
                probs = jnp.where(allowed, jnp.exp(scores - lse_ref[rows, :]), 0.0)
                prob_grad = contract_last(grad_rows, value_ref[keys, :])
                score_grad = (probs * (prob_grad - delta_ref[rows, :])).astype(jnp.bfloat16)
                value_acc[...] += contract_first(probs.astype(jnp.bfloat16), grad_rows)
                key_acc[...] += contract_first(score_grad, query)
                query_acc[rows, :] += jnp.dot(
                    score_grad, key_rows, preferred_element_type=jnp.float32
                )

        tables = (cos_ref[keys, :], low_ref[keys, :], high_ref[keys, :])
        key_low = turn(key_acc[:, :LANES] * score_scale, *tables, -1.0)
        key_high = key_acc[:, LANES:] * score_scale
        first = k_index == 0
        for start, part in ((HD, key_low), (HD + LANES, key_high), (2 * HD, value_acc[...])):
            columns = slice(start, start + part.shape[1])
            out_ref[keys, columns] = part.astype(jnp.bfloat16)
            sums_ref[:, columns] = jnp.where(first, 0.0, sums_ref[:, columns]) + jnp.sum(
                part, axis=0, keepdims=True
            )

    sums_ref[:, :HD] = jnp.zeros((1, HD), jnp.float32)

    @pl.loop(0, count)
    def _(q_index):
        rows = pl.ds(pl.multiple_of(q_index * block, block), block)
        tables = (cos_ref[rows, :], low_ref[rows, :], high_ref[rows, :])
        query_low = turn(query_acc[rows, :LANES] * score_scale, *tables, -1.0)
        query_high = query_acc[rows, LANES:] * score_scale
        for start, part in ((0, query_low), (LANES, query_high)):
            columns = slice(start, start + part.shape[1])
            out_ref[rows, columns] = part.astype(jnp.bfloat16)
            sums_ref[:, columns] += jnp.sum(part, axis=0, keepdims=True)


MESH = pl.DeviceIdType.MESH


def opening_kernel(*refs, side, second, ranks, square, sizes):
    count = len(sizes)
    gathered_in, refs = refs[:count], refs[count:]
    rows_in, refs = refs[:2], refs[2:]
    later_in, refs = refs[:2], refs[2:]
    gathered_out, refs = refs[:count], refs[count:]
    rows_out, refs = refs[:2], refs[2:]
    later_out, refs = refs[0], refs[1:]
    held, refs = refs[:count], refs[count:]
    held_rows, refs = refs[:2], refs[2:]
    held_later, refs = refs[:2], refs[2:]
    load_sem, store_sem, send_sem, recv_sem, row_send, row_recv = refs

    shard, rank = lax.axis_index("shard"), lax.axis_index("ctx")
    slow, fast = shard // second, shard % second
    flip = rank % 2 if square else 1
    here_first = fast * (1 - flip) + slow * flip
    here_second = slow * (1 - flip) + fast * flip

    def peer(first_step, second_step):
        first = (here_first + first_step + side) % side
        other = (here_second + second_step + second) % second
        return (other * side + first) * (1 - flip) + (first * second + other) * flip

    first_peers = [peer(a, 0) for a in range(1, side)]
    second_peers = [peer(0, b) for b in range(1, second)]
    rank_peers = [(rank + j) % ranks for j in range(1, ranks)]
    barrier = pltpu.get_barrier_semaphore()
    for target in first_peers + second_peers:
        pl.semaphore_signal(barrier, inc=1, device_id={"shard": target}, device_id_type=MESH)
    for target in rank_peers:
        pl.semaphore_signal(barrier, inc=1, device_id={"ctx": target}, device_id_type=MESH)

    loads = []
    for number in range(count):
        source = gathered_in[number]
        if sizes[number] is not None:
            columns = pl.ds(pl.multiple_of(rank * sizes[number], LANES), sizes[number])
            source = source.at[:, columns]
        loads.append(pltpu.make_async_copy(source, held[number], load_sem.at[number]))
    for number in range(2):
        loads.append(
            pltpu.make_async_copy(rows_in[number], held_rows[number], load_sem.at[count + number])
        )
    for number in range(2):
        size = held_later[number].shape[1]
        columns = pl.ds(pl.multiple_of(rank * size, LANES), size)
        loads.append(
            pltpu.make_async_copy(
                later_in[number].at[:, columns], held_later[number], load_sem.at[count + 2 + number]
            )
        )
    for load in loads:
        load.start()
    pl.semaphore_wait(barrier, len(first_peers) + len(second_peers) + len(rank_peers))

    def place(number, first_step, second_step):
        rows = held[number].shape[0]
        start = pl.multiple_of(peer(first_step, second_step) * rows, 16)
        return gathered_out[number].at[pl.ds(start, rows), :]

    copies, slot = {}, 0
    steps = side - 1 + (second - 1) * side

    def send(number, source, a, b, target, key):
        slot = number * steps + key
        copy = pltpu.make_async_remote_copy(
            src_ref=source,
            dst_ref=place(number, a, b),
            send_sem=send_sem.at[slot],
            recv_sem=recv_sem.at[slot],
            device_id={"shard": target},
            device_id_type=MESH,
        )
        copy.start()
        copies[number, key] = copy

    for number in range(count):
        loads[number].wait()
        for a in range(1, side):
            send(number, held[number], 0, 0, first_peers[a - 1], a - 1)
        for b in range(1, second):
            send(number, held[number], 0, 0, second_peers[b - 1], side - 1 + (b - 1) * side)
    row_copies = []
    for number in range(2):
        loads[count + number].wait()
        rows = held_rows[number].shape[0]
        for j in range(1, ranks):
            slot = number * (ranks - 1) + j - 1
            copy = pltpu.make_async_remote_copy(
                src_ref=held_rows[number],
                dst_ref=rows_out[number].at[pl.ds((ranks - j) * rows, rows), :],
                send_sem=row_send.at[slot],
                recv_sem=row_recv.at[slot],
                device_id={"ctx": rank_peers[j - 1]},
                device_id_type=MESH,
            )
            copy.start()
            row_copies.append(copy)
    stores = []
    for number in range(count):
        stores.append(
            pltpu.make_async_copy(held[number], place(number, 0, 0), store_sem.at[number])
        )
    for number in range(2):
        rows = held_rows[number].shape[0]
        stores.append(
            pltpu.make_async_copy(
                held_rows[number],
                rows_out[number].at[pl.ds(0, rows), :],
                store_sem.at[count + number],
            )
        )
    for number in range(2):
        loads[count + 2 + number].wait()
        size = held_later[number].shape[1]
        stores.append(
            pltpu.make_async_copy(
                held_later[number],
                later_out.at[:, pl.ds(number * size, size)],
                store_sem.at[count + 2 + number],
            )
        )
    for store in stores:
        store.start()
    for number in range(count):
        for a in range(1, side):
            copies[number, a - 1].wait_recv()
            for b in range(1, second):
                key = side - 1 + (b - 1) * side + a
                send(number, place(number, -a, 0), -a, 0, second_peers[b - 1], key)
    for store in stores:
        store.wait()
    for (number, key), copy in copies.items():
        copy.wait_send()
        if key >= side - 1:
            copy.wait_recv()
    for copy in row_copies:
        copy.wait_send()
        copy.wait_recv()


def opening(gathered, split, rows, later, ranks):
    shards = lax.axis_size("shard")
    side = math.isqrt(shards)
    square = side * side == shards
    if not square:
        side = 1
    second = shards // side
    sizes = [v.shape[1] // ranks if cut else None for v, cut in zip(gathered, split)]
    held = [(v.shape[0], size or v.shape[1]) for v, size in zip(gathered, sizes)]
    held_later = [(v.shape[0], v.shape[1] // ranks) for v in later]
    count, steps = len(gathered), side - 1 + (second - 1) * side
    bf16 = jnp.bfloat16
    out_shapes = (
        [jax.ShapeDtypeStruct((h[0] * shards, h[1]), bf16) for h in held]
        + [jax.ShapeDtypeStruct((v.shape[0] * ranks, v.shape[1]), bf16) for v in rows]
        + [jax.ShapeDtypeStruct((held_later[0][0], 2 * held_later[0][1]), bf16)]
    )
    hbm = pl.BlockSpec(memory_space=pl.ANY)
    total = count + 4
    row_slots = max(1, 2 * (ranks - 1))
    outs = pl.pallas_call(
        functools.partial(
            opening_kernel, side=side, second=second, ranks=ranks, square=square, sizes=sizes
        ),
        out_shape=tuple(out_shapes),
        in_specs=[hbm] * total,
        out_specs=(hbm,) * (total - 1),
        scratch_shapes=[pltpu.VMEM(h, bf16) for h in held]
        + [pltpu.VMEM(v.shape, bf16) for v in rows]
        + [pltpu.VMEM(h, bf16) for h in held_later]
        + [
            pltpu.SemaphoreType.DMA((total,)),
            pltpu.SemaphoreType.DMA((total,)),
            pltpu.SemaphoreType.DMA((count * steps,)),
            pltpu.SemaphoreType.DMA((count * steps,)),
            pltpu.SemaphoreType.DMA((row_slots,)),
            pltpu.SemaphoreType.DMA((row_slots,)),
        ],
        compiler_params=pltpu.CompilerParams(
            collective_id=0, has_side_effects=True, vmem_limit_bytes=VMEM_LIMIT
        ),
        name="opening",
    )(*gathered, *rows, *later)
    return outs[:count], outs[count : count + 2], outs[count + 2]


def pair_product_kernel(left_ref, right_ref, left_weight, right_weight, *refs):
    out_ref = refs[-1]
    out_ref[...] = (
        contract_last(left_ref[...], left_weight[...])
        + contract_last(right_ref[...], right_weight[...])
    ).astype(out_ref.dtype)


def block_sum_kernel(index_ref, whole_ref, *refs, count):
    del index_ref
    total = whole_ref[...].astype(jnp.float32)
    for ref in refs[:count]:
        total = total + ref[...].astype(jnp.float32)
    refs[-1][...] = total.astype(refs[-1].dtype)


def block_sum(whole, index, received, after, dtype):
    rows, columns = received[0].shape
    step = min(rows, 256)
    tiles = rows // step
    tile = pl.BlockSpec((step, columns), lambda i, index: (i, 0))
    return pl.pallas_call(
        functools.partial(block_sum_kernel, count=len(received)),
        grid_spec=pltpu.PrefetchScalarGridSpec(
            num_scalar_prefetch=1,
            grid=(tiles,),
            in_specs=[pl.BlockSpec((step, columns), lambda i, index: (index[0] * tiles + i, 0))]
            + [tile] * len(received)
            + [pl.BlockSpec(memory_space=pl.ANY)] * len(after),
            out_specs=tile,
        ),
        out_shape=jax.ShapeDtypeStruct((rows, columns), dtype),
        cost_estimate=pl.CostEstimate(
            flops=rows * columns, bytes_accessed=6 * rows * columns, transcendentals=0
        ),
        name="block_sum",
    )(jnp.asarray(index, jnp.int32).reshape(1), whole, *received, *after)


def norm_grad_kernel(
    left_ref,
    right_ref,
    x_ref,
    left_weight,
    right_weight,
    left_gain,
    right_gain,
    after_ref,
    out_ref,
    sums_ref,
):
    del after_ref
    x = x_ref[...].astype(jnp.float32)
    centered = x - jnp.mean(x, axis=-1, keepdims=True)
    inverse = lax.rsqrt(jnp.mean(centered * centered, axis=-1, keepdims=True) + EPSILON)
    hat = centered * inverse
    left = contract_last(left_ref[...], left_weight[...])
    right = contract_last(right_ref[...], right_weight[...])
    scaled = left * left_gain[...] + right * right_gain[...]
    first = pl.program_id(0) == 0
    for row, part in enumerate((left * hat, left, right * hat, right)):
        total = jnp.sum(part, axis=0, keepdims=True)
        sums_ref[row : row + 1, :] = jnp.where(first, 0.0, sums_ref[row : row + 1, :]) + total
    inner = (
        scaled
        - jnp.mean(scaled, axis=-1, keepdims=True)
        - hat * jnp.mean(scaled * hat, axis=-1, keepdims=True)
    )
    out_ref[...] = (inverse * inner).astype(out_ref.dtype)


ROWS_STEP = 256


def row_specs(arrays, start, rows):
    step = min(ROWS_STEP, rows)
    return step, [
        pl.BlockSpec((step, v.shape[1]), lambda i, first=start // step: (first + i, 0))
        for v in arrays
    ]


def whole_spec(array):
    return pl.BlockSpec(array.shape, lambda i: (0, 0))


def half_spec(array, half):
    return pl.BlockSpec((array.shape[0], array.shape[1] // 2), lambda i: (0, half))


def pair_product(left, right, left_weight, right_weight, after, start, rows):
    step, specs = row_specs((left, right), start, rows)
    width = left_weight.shape[0]
    return pl.pallas_call(
        pair_product_kernel,
        grid=(rows // step,),
        out_shape=jax.ShapeDtypeStruct((rows, width), jnp.bfloat16),
        in_specs=specs
        + [whole_spec(left_weight), half_spec(right_weight, 1)]
        + [pl.BlockSpec(memory_space=pl.ANY)] * len(after),
        out_specs=pl.BlockSpec((step, width), lambda i: (i, 0)),
        compiler_params=pltpu.CompilerParams(vmem_limit_bytes=VMEM_LIMIT),
        cost_estimate=pl.CostEstimate(
            flops=2 * rows * width * (left.shape[1] + right.shape[1]),
            bytes_accessed=2 * rows * (width + left.shape[1] + right.shape[1]),
            transcendentals=0,
        ),
        name="pair_product",
    )(left, right, left_weight, right_weight, *after)


def norm_grad(
    left, right, x, left_weight, right_weight, left_gain, right_gain, after, start, rows
):
    step, specs = row_specs((left, right, x), start, rows)
    width = left_weight.shape[0]
    rest = [left_weight, right_weight, left_gain, right_gain]
    return pl.pallas_call(
        norm_grad_kernel,
        grid=(rows // step,),
        out_shape=(
            jax.ShapeDtypeStruct((rows, width), jnp.bfloat16),
            jax.ShapeDtypeStruct((4, width), jnp.float32),
        ),
        in_specs=specs
        + [whole_spec(left_weight), half_spec(right_weight, 0)]
        + [whole_spec(v) for v in rest[2:]]
        + [pl.BlockSpec(memory_space=pl.ANY)],
        out_specs=(
            pl.BlockSpec((step, width), lambda i: (i, 0)),
            pl.BlockSpec((4, width), lambda i: (0, 0)),
        ),
        compiler_params=pltpu.CompilerParams(vmem_limit_bytes=VMEM_LIMIT),
        cost_estimate=pl.CostEstimate(
            flops=2 * rows * width * (left.shape[1] + right.shape[1]),
            bytes_accessed=2 * rows * (2 * width + left.shape[1] + right.shape[1]),
            transcendentals=0,
        ),
        name="norm_grad",
    )(left, right, x, *rest, after)


SCALAR = pl.BlockSpec(memory_space=pltpu.SMEM)
VECTOR = pl.BlockSpec(memory_space=pltpu.VMEM)


def attend(order, bounds, proj, tables, seg_col, seg_row, block, count):
    length = proj.shape[0]
    pairs = length * length
    return pl.pallas_call(
        functools.partial(attend_kernel, block=block, count=count),
        out_shape=(
            jax.ShapeDtypeStruct((length, HD), jnp.bfloat16),
            jax.ShapeDtypeStruct((length, HD), jnp.bfloat16),
            jax.ShapeDtypeStruct((length, HD), jnp.bfloat16),
            jax.ShapeDtypeStruct((length, HD), jnp.bfloat16),
            jax.ShapeDtypeStruct((length, 1), jnp.float32),
        ),
        in_specs=[SCALAR] * 2 + [VECTOR] * 6,
        out_specs=(VECTOR,) * 5,
        scratch_shapes=[
            pltpu.VMEM((block, 1), jnp.float32),
            pltpu.VMEM((block, 1), jnp.float32),
            pltpu.VMEM((block, HD), jnp.float32),
        ],
        compiler_params=pltpu.CompilerParams(vmem_limit_bytes=VMEM_LIMIT),
        cost_estimate=pl.CostEstimate(
            flops=2 * pairs * HD, bytes_accessed=16 * length * HD, transcendentals=pairs // 2
        ),
        name="attend",
    )(order, bounds, proj, *tables, seg_col, seg_row)


def attend_grad(
    order, bounds, query, key, value, attn, grad, lse, tables, seg_col, seg_row, block, count
):
    length = query.shape[0]
    pairs = length * length
    return pl.pallas_call(
        functools.partial(attend_grad_kernel, block=block, count=count),
        out_shape=(
            jax.ShapeDtypeStruct((length, 3 * HD), jnp.bfloat16),
            jax.ShapeDtypeStruct((1, 3 * HD), jnp.float32),
        ),
        in_specs=[SCALAR] * 2 + [VECTOR] * 11,
        out_specs=(VECTOR,) * 2,
        scratch_shapes=[
            pltpu.VMEM((length, HD), jnp.float32),
            pltpu.VMEM((block, HD), jnp.float32),
            pltpu.VMEM((block, HD), jnp.float32),
            pltpu.VMEM((length, 1), jnp.float32),
        ],
        compiler_params=pltpu.CompilerParams(vmem_limit_bytes=VMEM_LIMIT),
        cost_estimate=pl.CostEstimate(
            flops=5 * pairs * HD, bytes_accessed=16 * length * HD, transcendentals=pairs // 2
        ),
        name="attend_grad",
    )(order, bounds, query, key, value, attn, grad, lse, *tables, seg_col, seg_row)


def ring_shift(value, axis, step):
    count = lax.axis_size(axis)
    return lax.ppermute(value, axis, [(i, (i + step) % count) for i in range(count)])


class Plane:
    def __init__(self):
        self.count = lax.axis_size("shard")
        side = math.isqrt(self.count)
        self.square = side * side == self.count
        self.first, self.second = (side, side) if self.square else (1, self.count)
        self.ranks = lax.axis_size("ctx")
        shard = lax.axis_index("shard")
        self.flip = (lax.axis_index("ctx") % 2 == 1) if self.square else False
        slow, fast = shard // self.second, shard % self.second
        if self.square:
            self.here = (jnp.where(self.flip, slow, fast), jnp.where(self.flip, fast, slow))
        else:
            self.here = (slow, fast)

    def index(self, first_step, second_step):
        first = lax.rem(self.here[0] + first_step + self.first, self.first)
        second = lax.rem(self.here[1] + second_step + self.second, self.second)
        if not self.square:
            return first * self.second + second
        side = self.first
        return jnp.where(self.flip, first * side + second, second * side + first)

    def move(self, value, first_step, second_step):
        pairs = []
        for shard in range(self.count):
            for rank in range(self.ranks):
                slow, fast = divmod(shard, self.second)
                if self.square and rank % 2 == 0:
                    slow = (slow + second_step) % self.second
                    fast = (fast + first_step) % self.first
                else:
                    slow = (slow + first_step) % self.first
                    fast = (fast + second_step) % self.second
                target = slow * self.second + fast
                pairs.append((shard * self.ranks + rank, target * self.ranks + rank))
        return lax.ppermute(value, ("shard", "ctx"), pairs)

    def scatter_sum(self, partial, after):
        rows = partial.shape[0] // self.count
        sums, final = {}, []
        for b in list(range(1, self.second)) + [0]:
            received = []
            for a in range(1, self.first):
                block = lax.dynamic_slice_in_dim(partial, self.index(a, b) * rows, rows)
                received.append(self.move(block, a, 0))
            if b == 0:
                final = received
            elif received:
                sums[b] = block_sum(partial, self.index(0, b), received, after, partial.dtype)
            else:
                sums[b] = lax.dynamic_slice_in_dim(partial, self.index(0, b) * rows, rows)
        final = final + [self.move(sums[b], 0, b) for b in range(1, self.second)]
        return block_sum(partial, self.index(0, 0), final, after, jnp.float32)

    def full_sum(self, value):
        total = value
        for a in range(1, self.first):
            total = total + self.move(value, a, 0)
        value = total
        for b in range(1, self.second):
            total = total + self.move(value, 0, b)
        return total


def local(
    hidden_in,
    grad_out,
    segment_ids,
    group_order,
    ln1_gain,
    ln1_bias,
    qkv_weight,
    qkv_bias,
    dense_weight,
    dense_bias,
    ln2_gain,
    ln2_bias,
    up_weight,
    up_bias,
    down_weight,
    down_bias,
):
    _, groups_dev, block_len, width = hidden_in.shape
    tokens = groups_dev * block_len
    seq_len = segment_ids.shape[1]
    groups = seq_len // block_len
    ctx_count, tp_count = lax.axis_size("ctx"), lax.axis_size("tp")
    shard_count = lax.axis_size("shard")
    ctx_rank, tp_rank = lax.axis_index("ctx"), lax.axis_index("tp")
    shard_rank = lax.axis_index("shard")
    slice_width = width // tp_count
    bf16, f32 = jnp.bfloat16, jnp.float32

    def my_columns(matrix):
        columns = matrix.shape[1] // ctx_count
        return lax.dynamic_slice_in_dim(matrix, ctx_rank * columns, columns, 1)

    plane = Plane()

    x_mine = hidden_in.reshape(tokens, width)
    g_mine = grad_out.reshape(tokens, width)
    vectors = [
        ln1_gain, ln1_bias, ln2_gain, ln2_bias, dense_bias, down_bias, qkv_bias[0], up_bias[0],
    ]
    sizes = [v.shape[0] for v in vectors]
    wide = -(-max(sizes) // LANES) * LANES
    packed = jnp.stack([jnp.pad(v, (0, wide - v.shape[0])) for v in vectors])
    packed = jnp.concatenate([packed, jnp.zeros_like(packed)], axis=0)
    (w_vectors, w_qkv, w_dense), (x_row, g_row), wide_mine = opening(
        [packed, qkv_weight, dense_weight],
        [False, True, True],
        [x_mine, g_mine],
        [up_weight, down_weight],
        ctx_count,
    )
    w_wide = lax.all_gather(wide_mine, "shard", axis=0, tiled=True)
    units = w_wide.shape[1] // 2
    w_up, w_down = w_wide[:, :units], w_wide[:, units:]
    w_vectors = w_vectors.reshape(shard_count, packed.shape[0], wide)
    spread = [
        w_vectors[:, number, :size].reshape(-1).astype(f32) for number, size in enumerate(sizes)
    ]
    gain_one, shift_one, gain_two, shift_two, bias_dense, bias_down, bias_qkv, bias_up = spread
    bias_qkv = my_columns(bias_qkv[None])
    bias_up = my_columns(bias_up[None])
    plane = Plane()
    heads_here = w_qkv.shape[1] // (3 * HD)

    own_order = jnp.concatenate(
        [
            lax.dynamic_slice_in_dim(
                group_order, lax.rem(ctx_rank + k, ctx_count) * groups_dev, groups_dev
            )
            for k in range(ctx_count)
        ]
    )
    segments = segment_ids[0]
    positions = segment_positions(segments)

    def stored(values):
        return jnp.concatenate(
            [
                lax.dynamic_slice_in_dim(values, own_order[k] * block_len, block_len)
                for k in range(groups)
            ]
        )

    seg_stored = stored(segments)
    tables = rotary_tables(stored(positions))
    seg_blocks = seg_stored.reshape(groups, block_len)
    bounds = jnp.stack([seg_blocks[:, 0], seg_blocks[:, -1]])
    seg_col, seg_row = seg_stored[:, None], seg_stored[None, :]

    x_float = x_row.astype(f32)
    centered = x_float - jnp.mean(x_float, axis=-1, keepdims=True)
    inverse = lax.rsqrt(jnp.mean(centered * centered, axis=-1, keepdims=True) + EPSILON)
    hat = centered * inverse
    acts_one = (hat * gain_one + shift_one).astype(bf16)
    acts_two = (hat * gain_two + shift_two).astype(bf16)

    projected = jnp.dot(acts_one, w_qkv, preferred_element_type=f32) + bias_qkv
    heads = []
    for h in range(heads_here):
        heads.append(
            attend(
                own_order,
                bounds,
                projected[:, 3 * HD * h : 3 * HD * (h + 1)],
                tables,
                seg_col,
                seg_row,
                block_len,
                groups,
            )
        )
    attn = jnp.concatenate([head[3] for head in heads], axis=1)

    attn_grad = jnp.dot(g_row, w_dense, preferred_element_type=f32).astype(bf16)
    proj_parts, sum_parts = [], []
    for h, (query, key, value, attn_head, lse) in enumerate(heads):
        part, sums = attend_grad(
            own_order,
            bounds,
            query,
            key,
            value,
            attn_head,
            attn_grad[:, HD * h : HD * (h + 1)],
            lse,
            tables,
            seg_col,
            seg_row,
            block_len,
            groups,
        )
        proj_parts.append(part)
        sum_parts.append(sums[0])
    proj_grad_b = jnp.concatenate(proj_parts, axis=1)
    qkv_bias_grad = jnp.concatenate(sum_parts)

    pre_act = jnp.dot(acts_two, w_up, preferred_element_type=f32) + bias_up
    cdf = 0.5 * (1.0 + lax.erf(pre_act * (1.0 / math.sqrt(2.0))))
    hidden = (pre_act * cdf).astype(bf16)
    slope = cdf + pre_act * jnp.exp(-0.5 * pre_act * pre_act) * (1.0 / math.sqrt(2.0 * math.pi))

    def reduce_partial(parts):
        received = [ring_shift(parts[k], "ctx", k) for k in range(1, ctx_count)]
        total = block_sum(parts[0], 0, received, [], bf16)
        return total, lax.psum_scatter(total, "tp", scatter_dimension=1, tiled=True).astype(f32)

    out_parts = {}
    for k in reversed(range(ctx_count)):
        out_parts[k] = pair_product(
            attn,
            hidden,
            w_dense,
            w_wide,
            [proj_grad_b] if k + 1 == ctx_count else [out_parts[k + 1]],
            k * tokens,
            tokens,
        )
    out_total, summed_out = reduce_partial(out_parts)
    out_shift = lax.dynamic_slice_in_dim(bias_dense + bias_down, tp_rank * slice_width, slice_width)
    x_slice = lax.dynamic_slice_in_dim(x_mine, tp_rank * slice_width, slice_width, 1)
    output = x_slice.astype(f32) + summed_out + out_shift

    def reduce_weight(grad, after):
        mine = plane.scatter_sum(grad, after)
        rows, columns = mine.shape
        whole = jnp.zeros((rows, columns * ctx_count), f32)
        for k in range(ctx_count):
            part = mine if k == 0 else ring_shift(mine.astype(bf16), "ctx", ctx_count - k)
            place = lax.rem(ctx_rank + k, ctx_count) * columns
            whole = lax.dynamic_update_slice_in_dim(whole, part.astype(f32), place, 1)
        return whole

    bias_grad = jnp.sum(g_row.astype(f32), axis=0)

    pre_grad = jnp.dot(g_row, w_down, preferred_element_type=f32) * slope
    up_bias_grad = jnp.sum(pre_grad, axis=0)
    pre_grad_b = pre_grad.astype(bf16)

    in_parts, norm_sums = {}, jnp.zeros((4, width), f32)
    for k in reversed(range(ctx_count)):
        in_parts[k], sums = norm_grad(
            proj_grad_b,
            pre_grad_b,
            x_row,
            w_qkv,
            w_wide,
            gain_one[None],
            gain_two[None],
            in_parts[k + 1] if k + 1 in in_parts else out_total,
            k * tokens,
            tokens,
        )
        norm_sums = norm_sums + sums
    _, input_sum = reduce_partial(in_parts)
    g_slice = lax.dynamic_slice_in_dim(g_mine, tp_rank * slice_width, slice_width, 1)
    input_grad = g_slice.astype(f32) + input_sum

    down_local = contract_first(g_row, hidden).astype(bf16)
    dense_local = contract_first(g_row, attn).astype(bf16)
    qkv_local = contract_first(acts_one, proj_grad_b).astype(bf16)
    up_local = contract_first(acts_two, pre_grad_b).astype(bf16)
    late = [dense_local, qkv_local, up_local]
    down_grad = reduce_weight(down_local, [in_parts[0]])
    dense_grad = reduce_weight(dense_local, late)
    qkv_grad = reduce_weight(qkv_local, late)
    up_grad = reduce_weight(up_local, late)

    norm_sums = norm_sums.reshape(-1)
    column_sums = [up_bias_grad, qkv_bias_grad]
    packed = jnp.concatenate([norm_sums] + column_sums)
    wholes = [jnp.zeros((v.shape[0] * ctx_count,), f32) for v in column_sums]
    total = jnp.zeros_like(norm_sums)
    for k in range(ctx_count):
        part = packed if k == 0 else ring_shift(packed, "ctx", ctx_count - k)
        total = total + part[: norm_sums.shape[0]]
        offset = norm_sums.shape[0]
        for number, vector in enumerate(column_sums):
            size = vector.shape[0]
            wholes[number] = lax.dynamic_update_slice_in_dim(
                wholes[number],
                part[offset : offset + size],
                lax.rem(ctx_rank + k, ctx_count) * size,
                0,
            )
            offset += size
    norm_sums = total
    for k in range(1, tp_count):
        norm_sums = norm_sums + ring_shift(total, "tp", k)
    pieces = [bias_grad] + wholes + [
        norm_sums[k * width : (k + 1) * width] for k in range(4)
    ]
    reduced = plane.full_sum(jnp.concatenate(pieces))
    results, offset = [], 0
    for piece in pieces:
        own = piece.shape[0] // shard_count
        results.append(lax.dynamic_slice_in_dim(reduced, offset + shard_rank * own, own))
        offset += piece.shape[0]
    bias_grad, up_bias_grad, qkv_bias_grad = results[:3]
    gain_one_grad, shift_one_grad, gain_two_grad, shift_two_grad = results[3:]
    out_shape = hidden_in.shape[:3] + (slice_width,)
    return (
        output.reshape(out_shape),
        input_grad.reshape(out_shape),
        gain_one_grad,
        shift_one_grad,
        qkv_grad,
        qkv_bias_grad[None],
        dense_grad,
        bias_grad,
        gain_two_grad,
        shift_two_grad,
        up_grad,
        up_bias_grad[None],
        down_grad,
    )


def solution(mesh):
    return jax.shard_map(
        local,
        mesh=mesh,
        in_specs=(
            P("shard", "ctx", None, None),
            P("shard", "ctx", None, None),
            P("shard", None),
            P(),
            P("shard"),
            P("shard"),
            P("shard", "tp"),
            P("tp", "shard"),
            P("shard", "tp"),
            P("shard"),
            P("shard"),
            P("shard"),
            P("shard", "tp"),
            P("tp", "shard"),
            P("shard", "tp"),
            P("shard"),
        ),
        out_specs=(
            P("shard", "ctx", None, "tp"),
            P("shard", "ctx", None, "tp"),
            P("shard"),
            P("shard"),
            P("shard", "tp"),
            P("tp", "shard"),
            P("shard", "tp"),
            P("shard"),
            P("shard"),
            P("shard"),
            P("shard", "tp"),
            P("tp", "shard"),
            P("shard", "tp"),
        ),
        check_vma=False,
    )
```

profile of v0, /device:TPU:0, one launch (start us, length us, event | category | flops | bytes accessed | tf_op | source)
XLA Modules:
  0.0 425.8 jit_solution(4782673807603958420)
XLA Ops:
  12.0 1.9 concatenate.39.refs_0_
  14.0 39.6 %opening.1 = (bf16[64,512]{1,0:T(8,128)(2,1)}, bf16[2048,768]{1,0:T(8,128)(2,1)}, bf16[2048,256]{1,0:T(8,128)(2,1)}, bf16[2048,2048]{1,0:T(8,128)(2,1)}, bf16[20...) custom-call(bf16[16,512]{1,0:T(8,128)(2,1)} %concatenate.39.refs_0_, bf16[512,1536]{1,0:T(8,128)(2,1)} %refs_1_.1, ...), custom_call_target="tpu_custom_call" | custom-call | tf_op jit(solution)/shard_map/opening/pallas_call | solution.py:392
  59.6 1.3 copy.36.seg_col_ref
  61.3 3.7 multiply_sine_fusion
  67.5 4.7 %convert_reduce_fusion = f32[2048]{0:T(1024)S(1)} fusion(bf16[2048,2048]{1,0:T(8,128)(2,1)} %get-tuple-element.30.x_ref), kind=kLoop, calls=%fused_computation.1 | loop fusion | flops 8386560 | bytes 8396800 | tf_op jit(solution)/shard_map/reduce_sum | solution.py:778
  72.2 5.8 %fusion.8 = f32[2048]{0:T(1024)S(1)} fusion(bf16[2048,2048]{1,0:T(8,128)(2,1)} %get-tuple-element.30.x_ref, f32[2048]{0:T(1024)S(1)} %broadcast_multiply_fusion), kind=kLoop, calls=%fused_computation.10 | loop fusion | flops 16775168 | bytes 8404992 | tf_op jit(solution)/shard_map/reduce_sum | solution.py:779
  78.0 1.3 maximum_maximum_fusion.cos_ref
  79.3 1.3 maximum_maximum_fusion.1.high_ref
  80.7 3.9 fusion.5
  84.6 8.5 %broadcast_add_fusion.proj_ref = f32[2048,768]{1,0:T(8,128)} fusion(f32[768]{0:T(1024)S(1)} %dynamic-slice.10, bf16[2048,2048]{1,0:T(8,128)(2,1)S(1)} %fusion.5, bf16[2048,768]{1,0:T(8,128)(2,1)S(1)} %copy-done.5), kind=kOutput, calls=%fused_computation.26 | convolution fusion | flops 6444023808 | bytes 17828864 | tf_op jit(solution)/shard_map/dot_general | solution.py:784
  93.1 19.3 %attend.1 = (bf16[2048,256]{1,0:T(8,128)(2,1)}, bf16[2048,256]{1,0:T(8,128)(2,1)}, bf16[2048,256]{1,0:T(8,128)(2,1)}, bf16[2048,256]{1,0:T(8,128)(2,1)}, f32[2048,1]{1,0:T(8,128)}) custom-call(s32[4]{0:T(128)} %pad_add_fusion.2.order_ref, s32[2,4]{1,0:T(2,128)} %pad_add_fusion.1.bounds_ref, f32[2048,768]{1,0:T(8,128)} %broadcast_add_fusion.proj_ref, ...), custom_call_target="tpu_custom_call" | custom-call | flops 2147483648 | bytes 8388608 | tf_op jit(solution)/shard_map/attend/pallas_call | solution.py:567
  112.4 6.7 %convolution_convert_fusion.4.grad_ref = bf16[2048,256]{1,0:T(8,128)(2,1)} fusion(bf16[2048,2048]{1,0:T(8,128)(2,1)} %get-tuple-element.39, bf16[2048,256]{1,0:T(8,128)(2,1)S(1)} %copy-done.7), kind=kOutput, calls=%fused_computation.28 | convolution fusion | flops 2148007936 | bytes 10485760 | tf_op jit(solution)/shard_map/dot_general | solution.py:801
  119.1 17.4 %attend_grad.1 = (bf16[2048,768]{1,0:T(8,128)(2,1)}, f32[1,768]{1,0:T(1,128)}) custom-call(s32[4]{0:T(128)} %pad_add_fusion.2.order_ref, s32[2,4]{1,0:T(2,128)} %pad_add_fusion.1.bounds_ref, bf16[2048,256]{1,0:T(8,128)(2,1)} %get-tuple-element.36.query_ref, bf16[2048,256]{1,0:T(8,128)(2,1)} %get-tuple-element.37.key_ref, ...), custom_call_target="tpu_custom_call" | custom-call | flops 5368709120 | bytes 8388608 | tf_op jit(solution)/shard_map/attend_grad/pallas_call | solution.py:596
  136.5 5.0 %all-gather.2.cloned.1.call-done.right_weight = bf16[2048,2048]{1,0:T(8,128)(2,1)} async-done(((bf16[512,2048]{1,0:T(8,128)(2,1)}), bf16[2048,2048]{1,0:T(8,128)(2,1)}) %all-gather.2.cloned.1.call-update) | async-done | bytes 8388624 | tf_op jit(solution)/shard_map/all_gather | solution.py:739
  141.5 16.2 %multiply_convert_fusion = (bf16[2048,1024]{1,0:T(8,128)(2,1)}, f32[2048,1024]{1,0:T(8,128)}) fusion(f32[1024]{0:T(1024)S(1)} %dynamic-slice.11, bf16[2048,2048]{1,0:T(8,128)(2,1)} %all-gather.2.cloned.1.call-done.right_weight, bf16[2048,2048]{1,0:T(8,128)(2,1)} %get-tuple-element.30.x_ref, f32[2048]{0:T(1024)S(1)} %bitcast.85, f32[2048]{0:T(1024)S(1)} %bitcast.87, ...), kind=kOutput, calls=%fused_computation.18 | convolution fusion | flops 8627683328 | bytes 25202688 | tf_op jit(solution)/shard_map/dot_general | solution.py:824
  157.6 10.0 %pair_product.2.refs_0_ = bf16[1024,2048]{1,0:T(8,128)(2,1)} custom-call(bf16[2048,256]{1,0:T(8,128)(2,1)} %get-tuple-element.33.attn_ref.left_ref, bf16[2048,1024]{1,0:T(8,128)(2,1)} %get-tuple-element.99.right_ref, bf16[2048,256]{1,0:T(8,128)(2,1)} %get-tuple-element.35.left_weight, bf16[2048,2048]{1,0:T(8,128)(2,1)} %all-gather.2.cloned.1.call-done.right_weight, ...), custom_call_target="tpu_custom_call" | custom-call | flops 5368709120 | bytes 6815744 | tf_op jit(solution)/shard_map/pair_product/pallas_call | solution.py:511
  167.6 10.0 %pair_product.3.whole_ref = bf16[1024,2048]{1,0:T(8,128)(2,1)} custom-call(bf16[2048,256]{1,0:T(8,128)(2,1)} %get-tuple-element.33.attn_ref.left_ref, bf16[2048,1024]{1,0:T(8,128)(2,1)} %get-tuple-element.99.right_ref, bf16[2048,256]{1,0:T(8,128)(2,1)} %get-tuple-element.35.left_weight, bf16[2048,2048]{1,0:T(8,128)(2,1)} %all-gather.2.cloned.1.call-done.right_weight, ...), custom_call_target="tpu_custom_call" | custom-call | flops 5368709120 | bytes 6815744 | tf_op jit(solution)/shard_map/pair_product/pallas_call | solution.py:511
  177.7 6.0 %block_sum.10.after_ref = bf16[1024,2048]{1,0:T(8,128)(2,1)} custom-call(s32[1]{0:T(128)} %constant.113.clone.1.index_ref, bf16[1024,2048]{1,0:T(8,128)(2,1)} %pair_product.3.whole_ref, bf16[1024,2048]{1,0:T(8,128)(2,1)} %collective-permute-done.refs_0_), custom_call_target="tpu_custom_call" | custom-call | flops 2097152 | bytes 12582912 | tf_op jit(solution)/shard_map/block_sum/pallas_call | solution.py:439
  185.0 17.5 %fusion.23 = (f32[1024]{0:T(1024)S(1)}, bf16[2048,1024]{1,0:T(8,128)(2,1)}) fusion(f32[2048,1024]{1,0:T(8,128)} %get-tuple-element.100, f32[1024]{0:T(1024)S(1)} %dynamic-slice.11, bf16[2048,2048]{1,0:T(8,128)(2,1)} %get-tuple-element.39, bf16[2048,2048]{1,0:T(8,128)(2,1)} %all-gather.2.cloned.1.call-done.right_weight), kind=kOutput, calls=%fused_computation.90 | convolution fusion | flops 8615099392 | bytes 25174016 | tf_op jit(solution)/shard_map/dot_general | solution.py:862
  202.5 17.6 %norm_grad.2 = (bf16[1024,2048]{1,0:T(8,128)(2,1)}, f32[4,2048]{1,0:T(4,128)}) custom-call(bf16[2048,768]{1,0:T(8,128)(2,1)} %get-tuple-element.41.refs_0_.left_ref, bf16[2048,1024]{1,0:T(8,128)(2,1)} %get-tuple-element.50.right_ref, bf16[2048,2048]{1,0:T(8,128)(2,1)} %get-tuple-element.30.x_ref, bf16[2048,768]{1,0:T(8,128)(2,1)} %get-tuple-element.32.left_weight, ...), custom_call_target="tpu_custom_call" | custom-call | flops 7516192768 | bytes 12058624 | tf_op jit(solution)/shard_map/norm_grad/pallas_call | solution.py:535
  220.6 6.0 %convolution_convert_fusion.3.refs_1_.refs_2_.whole_ref = bf16[2048,256]{1,0:T(8,128)(2,1)S(1)} fusion(bf16[2048,2048]{1,0:T(8,128)(2,1)} %get-tuple-element.39, bf16[2048,256]{1,0:T(8,128)(2,1)S(1)} %copy-done.8), kind=kOutput, calls=%fused_computation.27 | convolution fusion | flops 2148007936 | bytes 10485760 | tf_op jit(solution)/shard_map/dot_general | solution.py:56
  227.7 1.4 collective-permute-start.13
  229.2 9.6 %convolution_convert_fusion.2.whole_ref.refs_2_.refs_3_ = bf16[2048,768]{1,0:T(8,128)(2,1)S(1)} fusion(bf16[2048,2048]{1,0:T(8,128)(2,1)} %copy-done.6, bf16[2048,768]{1,0:T(8,128)(2,1)S(1)} %copy-done.3), kind=kOutput, calls=%fused_computation.25 | convolution fusion | flops 6444023808 | bytes 14680064 | tf_op jit(solution)/shard_map/dot_general | solution.py:56
  238.9 18.6 %norm_grad.3 = (bf16[1024,2048]{1,0:T(8,128)(2,1)}, f32[4,2048]{1,0:T(4,128)}) custom-call(bf16[2048,768]{1,0:T(8,128)(2,1)} %get-tuple-element.41.refs_0_.left_ref, bf16[2048,1024]{1,0:T(8,128)(2,1)} %get-tuple-element.50.right_ref, bf16[2048,2048]{1,0:T(8,128)(2,1)} %get-tuple-element.30.x_ref, bf16[2048,768]{1,0:T(8,128)(2,1)} %get-tuple-element.32.left_weight, ...), custom_call_target="tpu_custom_call" | custom-call | flops 7516192768 | bytes 12058624 | tf_op jit(solution)/shard_map/norm_grad/pallas_call | solution.py:535
  257.4 6.1 %block_sum.11 = bf16[1024,2048]{1,0:T(8,128)(2,1)} custom-call(s32[1]{0:T(128)} %constant.113.clone.1.index_ref, bf16[1024,2048]{1,0:T(8,128)(2,1)} %get-tuple-element.43.whole_ref.refs_1_.refs_2_, bf16[1024,2048]{1,0:T(8,128)(2,1)} %collective-permute-done.1.refs_0_), custom_call_target="tpu_custom_call" | custom-call | flops 2097152 | bytes 12582912 | tf_op jit(solution)/shard_map/block_sum/pallas_call | solution.py:439
  263.5 14.2 %convolution_convert_fusion.1.refs_3_.refs_4_.whole_ref = bf16[2048,1024]{1,0:T(8,128)(2,1)S(1)} fusion(bf16[2048,1024]{1,0:T(8,128)(2,1)} %get-tuple-element.50.right_ref, bf16[2048,2048]{1,0:T(8,128)(2,1)} %get-tuple-element.30.x_ref, f32[2048]{0:T(1024)S(1)} %bitcast.86, f32[2048]{0:T(1024)S(1)} %bitcast.88, f32[2048]{0:T(1024)S(1)} %add_rsqrt_fusion, ...), kind=kOutput, calls=%fused_computation.24 | convolution fusion | flops 8617197568 | bytes 16809984 | tf_op jit(solution)/shard_map/dot_general | solution.py:56
  277.7 2.0 copy-done
  279.7 1.5 constant_dynamic-slice_fusion.2
  281.7 1.2 constant_dynamic-slice_fusion.6
  282.9 1.5 collective-permute-start.9
  285.0 1.5 collective-permute-start.12
  286.5 1.8 block_sum.14
  288.7 4.8 %convert_reduce_fusion.1 = f32[2048]{0:T(1024)S(1)} fusion(bf16[2048,2048]{1,0:T(8,128)(2,1)} %get-tuple-element.39), kind=kLoop, calls=%fused_computation.11 | loop fusion | flops 8386560 | bytes 8396800 | tf_op jit(solution)/shard_map/reduce_sum | solution.py:860
  294.9 12.5 %collective-permute-done.9.refs_0_ = bf16[512,768]{1,0:T(8,128)(2,1)S(1)} collective-permute-done((bf16[512,768]{1,0:T(8,128)(2,1)}, bf16[512,768]{1,0:T(8,128)(2,1)S(1)}, u32[]{:S(2)}, u32[]{:S(2)}) %collective-permute-start.9) | collective-permute-done | bytes 786464 | tf_op jit(solution)/shard_map/ppermute | solution.py:659
  308.3 2.2 block_sum.12
  311.0 14.0 %collective-permute-done.12.refs_0_ = bf16[512,256]{1,0:T(8,128)(2,1)S(1)} collective-permute-done((bf16[512,256]{1,0:T(8,128)(2,1)S(1)}, bf16[512,256]{1,0:T(8,128)(2,1)S(1)}, u32[]{:S(2)}, u32[]{:S(2)}) %collective-permute-start.12) | collective-permute-done | bytes 262176 | tf_op jit(solution)/shard_map/ppermute | solution.py:659
  326.2 2.0 block_sum.15
  328.3 1.3 fusion.27
  329.7 2.5 block_sum.16
  332.2 1.4 collective-permute-start.18
  333.6 12.8 %convolution_convert_fusion.whole_ref = bf16[2048,1024]{1,0:T(8,128)(2,1)S(1)} fusion(bf16[2048,2048]{1,0:T(8,128)(2,1)} %get-tuple-element.39, bf16[2048,1024]{1,0:T(8,128)(2,1)} %get-tuple-element.99.right_ref), kind=kOutput, calls=%fused_computation.23 | convolution fusion | flops 8592031744 | bytes 16777216 | tf_op jit(solution)/shard_map/dot_general | solution.py:56
  346.7 1.7 copy-done.4
  348.4 1.6 constant_dynamic-slice_fusion
  350.6 1.5 collective-permute-start.21
  353.0 2.6 block_sum.13
  356.0 3.1 fusion.26
  359.1 3.0 block_sum.17
  362.3 2.5 broadcast.59.clone
  364.8 4.4 %fusion.25 = (bf16[512,1024]{1,0:T(8,128)(2,1)}, f32[512,2048]{1,0:T(8,128)}) fusion(f32[512,1024]{1,0:T(8,128)} %block_sum.17, f32[512,2048]{1,0:T(8,128)} %broadcast.59.clone, s32[]{:T(128)S(6)} %select_n.150), kind=kLoop, calls=%fused_computation.92 | loop fusion | flops 524288 | bytes 5242884 | tf_op jit(solution)/shard_map/convert_element_type | solution.py:855
  369.2 7.1 %collective-permute-done.21.refs_0_ = bf16[512,1024]{1,0:T(8,128)(2,1)} collective-permute-done((bf16[512,1024]{1,0:T(8,128)(2,1)}, bf16[512,1024]{1,0:T(8,128)(2,1)}, u32[]{:S(2)}, u32[]{:S(2)}) %collective-permute-start.21) | collective-permute-done | bytes 1048608 | tf_op jit(solution)/shard_map/ppermute | solution.py:659
  376.3 2.4 block_sum.18
  379.4 3.2 collective-permute-start.5
  382.6 1.1 collective-permute-start.3
  384.2 3.2 collective-permute-done.4
  388.3 1.6 collective-permute-start.6
  390.0 4.5 %collective-permute-done.22.refs_1_ = bf16[512,1024]{1,0:T(8,128)(2,1)} collective-permute-done((bf16[512,1024]{1,0:T(8,128)(2,1)}, bf16[512,1024]{1,0:T(8,128)(2,1)}, u32[]{:S(2)}, u32[]{:S(2)}) %collective-permute-start.22) | collective-permute-done | bytes 1048608 | tf_op jit(solution)/shard_map/ppermute | solution.py:659
  394.4 3.0 block_sum.19
  397.4 2.5 broadcast.59.clone.1
  399.9 4.0 fusion.24
  403.9 1.3 convert_dynamic-update-slice_fusion.2
  406.0 3.1 convert_dynamic-update-slice_fusion.1
  410.9 1.6 convert_dynamic-update-slice_fusion
  412.5 3.2 add_add_fusion
  415.7 3.2 convert_add_fusion
  (161 shorter events, 26.3 us)
Async XLA Ops:
  7.2 134.3 %all-gather.2.cloned.1.call-start = ((), (), s32[]{:S(2)}) async-start(), calls=%async_computation.2 | async-start | bytes 10485760 | tf_op jit(solution)/shard_map/all_gather | solution.py:739
  14.0 39.7 %copy-start.21 = (s32[4]{0:T(128)S(1)}, s32[4]{0:T(128)}, u32[]{:S(2)}) copy-start(s32[4]{0:T(128)} %param.19) | copy-start | bytes 52
  14.0 43.0 %copy-start.17 = (s32[1,2048]{1,0:T(1,128)S(1)}, s32[1,2048]{1,0:T(1,128)}, u32[]{:S(2)}) copy-start(s32[1,2048]{1,0:T(1,128)} %param.18) | copy-start | bytes 24580
  53.6 358.9 %reduce-scatter.3.cloned.1.call-start = ((), (), s32[]{:S(2)}) async-start(), calls=%async_computation.3 | async-start | bytes 5242880 | tf_op jit(solution)/shard_map/reduce_scatter | solution.py:832
  57.0 21.1 %copy-start.16 = (s32[2048]{0:T(1024)}, s32[2048]{0:T(1024)S(1)}, u32[]{:S(2)}) copy-start(s32[2048]{0:T(1024)S(1)} %pad_add_fusion) | copy-start | bytes 24580
  67.5 13.2 %slice-start = ((s8[8388608]{0:T(1024)(128)(4,1)}), s8[4194304]{0:T(1024)(128)(4,1)S(1)}, s32[]{:S(2)}) async-start(s8[8388608]{0:T(1024)(128)(4,1)} %bitcast.61), calls=%async_computation.5 | async-start | bytes 8388608
  72.2 8.5 %slice-start.1 = ((s8[8388608]{0:T(1024)(128)(4,1)}), s8[4194304]{0:T(1024)(128)(4,1)S(1)}, s32[]{:S(2)}) async-start(s8[8388608]{0:T(1024)(128)(4,1)} %bitcast.61), calls=%async_computation.6 | async-start | bytes 8388608
  80.7 3.9 copy-start.5
  84.6 8.5 %copy-start.6 = (bf16[2048,2048]{1,0:T(8,128)(2,1)}, bf16[2048,2048]{1,0:T(8,128)(2,1)S(1)}, u32[]{:S(2)}) copy-start(bf16[2048,2048]{1,0:T(8,128)(2,1)S(1)} %fusion.5) | copy-start | bytes 25165828
  93.1 19.3 %copy-start.7 = (bf16[2048,256]{1,0:T(8,128)(2,1)S(1)}, bf16[2048,256]{1,0:T(8,128)(2,1)}, u32[]{:S(2)}) copy-start(bf16[2048,256]{1,0:T(8,128)(2,1)} %get-tuple-element.35.left_weight) | copy-start | bytes 3145732
  167.6 10.0 %collective-permute-start = (bf16[1024,2048]{1,0:T(8,128)(2,1)}, bf16[1024,2048]{1,0:T(8,128)(2,1)}, u32[]{:S(2)}, u32[]{:S(2)}) collective-permute-start(bf16[1024,2048]{1,0:T(8,128)(2,1)} %pair_product.2.refs_0_), channel_id=1, source_target_pairs={{0,4},{4,0},{1,5},{5,1},{2,6},{6,2},{3,7},{7,3},{8,12},{12,8},{9,1... | collective-permute-start | bytes 12582920 | tf_op jit(solution)/shard_map/ppermute | solution.py:620
  183.7 232.0 %reduce-scatter.5.cloned.1.call-start = ((), (), s32[]{:S(2)}) async-start(), calls=%async_computation.4 | async-start | bytes 5242880 | tf_op jit(solution)/shard_map/reduce_scatter | solution.py:832
  202.5 18.1 %copy-start.8 = (bf16[2048,256]{1,0:T(8,128)(2,1)S(1)}, bf16[2048,256]{1,0:T(8,128)(2,1)}, u32[]{:S(2)}) copy-start(bf16[2048,256]{1,0:T(8,128)(2,1)} %get-tuple-element.33.attn_ref.left_ref) | copy-start | bytes 3145732
  220.1 37.3 %collective-permute-start.1 = (bf16[1024,2048]{1,0:T(8,128)(2,1)}, bf16[1024,2048]{1,0:T(8,128)(2,1)}, u32[]{:S(2)}, u32[]{:S(2)}) collective-permute-start(bf16[1024,2048]{1,0:T(8,128)(2,1)} %get-tuple-element.42.after_ref), channel_id=1, source_target_pairs={{0,4},{4,0},{1,5},{5,1},{2,6},{6,2},{3,7},{7,3},{8,12},{12,8},{9,1... | collective-permute-start | bytes 12582920 | tf_op jit(solution)/shard_map/ppermute | solution.py:620
  220.6 8.5 %copy-start.3 = (bf16[2048,768]{1,0:T(8,128)(2,1)S(1)}, bf16[2048,768]{1,0:T(8,128)(2,1)}, u32[]{:S(2)}) copy-start(bf16[2048,768]{1,0:T(8,128)(2,1)} %get-tuple-element.41.refs_0_.left_ref) | copy-start | bytes 9437188
  226.7 1.1 copy-start.2
  227.7 58.7 %collective-permute-start.13 = (bf16[512,256]{1,0:T(8,128)(2,1)}, bf16[512,256]{1,0:T(8,128)(2,1)}, u32[]{:S(2)}, u32[]{:S(2)}) collective-permute-start(bf16[512,256]{1,0:T(8,128)(2,1)} %get-tuple-element.63), channel_id=1, source_target_pairs={{0,8},{4,20},{8,0},{12,28},{16,24},{20,4},{24,16},{28,12},{1,9},{5... | collective-permute-start | bytes 786440 | tf_op jit(solution)/shard_map/ppermute | solution.py:659
  238.8 42.9 %copy-start.1 = (bf16[2048,768]{1,0:T(8,128)(2,1)}, bf16[2048,768]{1,0:T(8,128)(2,1)S(1)}, u32[]{:S(2)}) copy-start(bf16[2048,768]{1,0:T(8,128)(2,1)S(1)} %convolution_convert_fusion.2.whole_ref.refs_2_.refs_3_) | copy-start | bytes 9437188
  277.7 2.0 copy-start
  281.2 48.5 %collective-permute-start.17 = (bf16[512,1024]{1,0:T(8,128)(2,1)}, bf16[512,1024]{1,0:T(8,128)(2,1)}, u32[]{:S(2)}, u32[]{:S(2)}) collective-permute-start(bf16[512,1024]{1,0:T(8,128)(2,1)} %get-tuple-element.53), channel_id=1, source_target_pairs={{0,8},{4,20},{8,0},{12,28},{16,24},{20,4},{24,16},{28,12},{1,9},{5... | collective-permute-start | bytes 3145736 | tf_op jit(solution)/shard_map/ppermute | solution.py:659
  282.9 24.5 %collective-permute-start.9 = (bf16[512,768]{1,0:T(8,128)(2,1)}, bf16[512,768]{1,0:T(8,128)(2,1)S(1)}, u32[]{:S(2)}, u32[]{:S(2)}) collective-permute-start(bf16[512,768]{1,0:T(8,128)(2,1)} %get-tuple-element.55), channel_id=1, source_target_pairs={{0,8},{4,20},{8,0},{12,28},{16,24},{20,4},{24,16},{28,12},{1,9},{5... | collective-permute-start | bytes 2359304 | tf_op jit(solution)/shard_map/ppermute | solution.py:659
  284.5 66.1 %collective-permute-start.8 = (bf16[512,768]{1,0:T(8,128)(2,1)}, bf16[512,768]{1,0:T(8,128)(2,1)S(1)}, u32[]{:S(2)}, u32[]{:S(2)}) collective-permute-start(bf16[512,768]{1,0:T(8,128)(2,1)} %get-tuple-element.56), channel_id=1, source_target_pairs={{0,8},{4,20},{8,0},{12,28},{16,24},{20,4},{24,16},{28,12},{1,9},{5... | collective-permute-start | bytes 2359304 | tf_op jit(solution)/shard_map/ppermute | solution.py:659
  285.0 40.1 %collective-permute-start.12 = (bf16[512,256]{1,0:T(8,128)(2,1)S(1)}, bf16[512,256]{1,0:T(8,128)(2,1)S(1)}, u32[]{:S(2)}, u32[]{:S(2)}) collective-permute-start(bf16[512,256]{1,0:T(8,128)(2,1)S(1)} %get-tuple-element.64), channel_id=1, source_target_pairs={{0,8},{4,20},{8,0},{12,28},{16,24},{20,4},{24,16},{28,12},{1,9},{5... | collective-permute-start | bytes 786440 | tf_op jit(solution)/shard_map/ppermute | solution.py:659
  286.5 8.1 %copy-start.20 = (f32[1,768]{1,0:T(1,128)S(1)}, f32[1,768]{1,0:T(1,128)}, u32[]{:S(2)}) copy-start(f32[1,768]{1,0:T(1,128)} %get-tuple-element.46) | copy-start | bytes 9220
  288.3 37.3 %collective-permute-start.14 = (bf16[512,256]{1,0:T(8,128)(2,1)}, bf16[512,256]{1,0:T(8,128)(2,1)S(1)}, u32[]{:S(2)}, u32[]{:S(2)}) collective-permute-start(bf16[512,256]{1,0:T(8,128)(2,1)} %block_sum.14), channel_id=1, source_target_pairs={{0,16},{4,12},{8,24},{12,4},{16,0},{20,28},{24,8},{28,20},{1,17},{... | collective-permute-start | bytes 786440 | tf_op jit(solution)/shard_map/ppermute | solution.py:659
  307.4 0.9 copy-start.13
  310.5 41.6 %collective-permute-start.10 = (bf16[512,768]{1,0:T(8,128)(2,1)}, bf16[512,768]{1,0:T(8,128)(2,1)S(1)}, u32[]{:S(2)}, u32[]{:S(2)}) collective-permute-start(bf16[512,768]{1,0:T(8,128)(2,1)} %block_sum.12), channel_id=1, source_target_pairs={{0,16},{4,12},{8,24},{12,4},{16,0},{20,28},{24,8},{28,20},{1,17},{... | collective-permute-start | bytes 2359304 | tf_op jit(solution)/shard_map/ppermute | solution.py:659
  325.0 0.7 copy-start.14
  325.0 34.1 %collective-permute-start.16 = (bf16[512,1024]{1,0:T(8,128)(2,1)}, bf16[512,1024]{1,0:T(8,128)(2,1)}, u32[]{:S(2)}, u32[]{:S(2)}) collective-permute-start(bf16[512,1024]{1,0:T(8,128)(2,1)} %get-tuple-element.54), channel_id=1, source_target_pairs={{0,8},{4,20},{8,0},{12,28},{16,24},{20,4},{24,16},{28,12},{1,9},{5... | collective-permute-start | bytes 3145736 | tf_op jit(solution)/shard_map/ppermute | solution.py:659
  325.5 0.7 copy-start.15
  329.6 20.3 %collective-permute-start.15 = (bf16[512,256]{1,0:T(8,128)(2,1)S(1)}, bf16[512,256]{1,0:T(8,128)(2,1)S(1)}, u32[]{:S(2)}, u32[]{:S(2)}) collective-permute-start(bf16[512,256]{1,0:T(8,128)(2,1)S(1)} %get-tuple-element.65), channel_id=1, source_target_pairs={{0,4},{4,0},{1,5},{5,1},{2,6},{6,2},{3,7},{7,3},{8,12},{12,8},{9,1... | collective-permute-start | bytes 786440 | tf_op jit(solution)/shard_map/ppermute | solution.py:620
  332.2 26.9 %collective-permute-start.18 = (bf16[512,1024]{1,0:T(8,128)(2,1)}, bf16[512,1024]{1,0:T(8,128)(2,1)}, u32[]{:S(2)}, u32[]{:S(2)}) collective-permute-start(bf16[512,1024]{1,0:T(8,128)(2,1)} %block_sum.16), channel_id=1, source_target_pairs={{0,16},{4,12},{8,24},{12,4},{16,0},{20,28},{24,8},{28,20},{1,17},{... | collective-permute-start | bytes 3145736 | tf_op jit(solution)/shard_map/ppermute | solution.py:659
  346.3 2.0 copy-start.4
  349.9 40.0 %collective-permute-start.20 = (bf16[512,1024]{1,0:T(8,128)(2,1)}, bf16[512,1024]{1,0:T(8,128)(2,1)}, u32[]{:S(2)}, u32[]{:S(2)}) collective-permute-start(bf16[512,1024]{1,0:T(8,128)(2,1)} %get-tuple-element.52), channel_id=1, source_target_pairs={{0,8},{4,20},{8,0},{12,28},{16,24},{20,4},{24,16},{28,12},{1,9},{5... | collective-permute-start | bytes 3145736 | tf_op jit(solution)/shard_map/ppermute | solution.py:659
  350.6 1.5 copy-start.10
  350.6 1.5 copy-start.11
  350.6 25.7 %collective-permute-start.21 = (bf16[512,1024]{1,0:T(8,128)(2,1)}, bf16[512,1024]{1,0:T(8,128)(2,1)}, u32[]{:S(2)}, u32[]{:S(2)}) collective-permute-start(bf16[512,1024]{1,0:T(8,128)(2,1)} %get-tuple-element.51), channel_id=1, source_target_pairs={{0,8},{4,20},{8,0},{12,28},{16,24},{20,4},{24,16},{28,12},{1,9},{5... | collective-permute-start | bytes 3145736 | tf_op jit(solution)/shard_map/ppermute | solution.py:659
  352.1 0.9 copy-start.12
  359.1 3.0 copy-start.18
  359.1 3.0 copy-start.19
  362.2 17.2 %collective-permute-start.2 = (f32[9984]{0:T(1024)S(1)}, f32[9984]{0:T(1024)S(1)}, u32[]{:S(2)}, u32[]{:S(2)}) collective-permute-start(f32[9984]{0:T(1024)S(1)} %pad_maximum_fusion.1), channel_id=1, source_target_pairs={{0,4},{4,0},{1,5},{5,1},{2,6},{6,2},{3,7},{7,3},{8,12},{12,8},{9,1... | collective-permute-start | bytes 119816 | tf_op jit(solution)/shard_map/ppermute | solution.py:620
  378.7 15.7 %collective-permute-start.22 = (bf16[512,1024]{1,0:T(8,128)(2,1)}, bf16[512,1024]{1,0:T(8,128)(2,1)}, u32[]{:S(2)}, u32[]{:S(2)}) collective-permute-start(bf16[512,1024]{1,0:T(8,128)(2,1)} %block_sum.18), channel_id=1, source_target_pairs={{0,16},{4,12},{8,24},{12,4},{16,0},{20,28},{24,8},{28,20},{1,17},{... | collective-permute-start | bytes 3145736 | tf_op jit(solution)/shard_map/ppermute | solution.py:659
  379.4 4.8 %collective-permute-start.5 = (f32[8192]{0:T(1024)S(1)}, f32[8192]{0:T(1024)S(1)}, u32[]{:S(2)}, u32[]{:S(2)}) collective-permute-start(f32[8192]{0:T(1024)S(1)} %slice_add_fusion), channel_id=1, source_target_pairs={{0,3},{1,0},{2,1},{3,2},{4,7},{5,4},{6,5},{7,6},{8,11},{9,8},{10,9... | collective-permute-start | bytes 98312 | tf_op jit(solution)/shard_map/ppermute | solution.py:620
  382.6 4.8 %collective-permute-start.4 = (f32[8192]{0:T(1024)S(1)}, f32[8192]{0:T(1024)S(1)}, u32[]{:S(2)}, u32[]{:S(2)}) collective-permute-start(f32[8192]{0:T(1024)S(1)} %slice_add_fusion), channel_id=1, source_target_pairs={{0,2},{1,3},{2,0},{3,1},{4,6},{5,7},{6,4},{7,5},{8,10},{9,11},{10,... | collective-permute-start | bytes 98312 | tf_op jit(solution)/shard_map/ppermute | solution.py:620
  382.6 5.7 %collective-permute-start.3 = (f32[8192]{0:T(1024)S(1)}, f32[8192]{0:T(1024)S(1)}, u32[]{:S(2)}, u32[]{:S(2)}) collective-permute-start(f32[8192]{0:T(1024)S(1)} %slice_add_fusion), channel_id=1, source_target_pairs={{0,1},{1,2},{2,3},{3,0},{4,5},{5,6},{6,7},{7,4},{8,9},{9,10},{10,1... | collective-permute-start | bytes 98312 | tf_op jit(solution)/shard_map/ppermute | solution.py:620
  384.2 19.8 %collective-permute-start.11 = (bf16[512,768]{1,0:T(8,128)(2,1)}, bf16[512,768]{1,0:T(8,128)(2,1)}, u32[]{:S(2)}, u32[]{:S(2)}) collective-permute-start(bf16[512,768]{1,0:T(8,128)(2,1)} %get-tuple-element.61), channel_id=1, source_target_pairs={{0,4},{4,0},{1,5},{5,1},{2,6},{6,2},{3,7},{7,3},{8,12},{12,8},{9,1... | collective-permute-start | bytes 2359304 | tf_op jit(solution)/shard_map/ppermute | solution.py:620
  387.4 18.6 %collective-permute-start.19 = (bf16[512,1024]{1,0:T(8,128)(2,1)}, bf16[512,1024]{1,0:T(8,128)(2,1)}, u32[]{:S(2)}, u32[]{:S(2)}) collective-permute-start(bf16[512,1024]{1,0:T(8,128)(2,1)} %get-tuple-element.59), channel_id=1, source_target_pairs={{0,4},{4,0},{1,5},{5,1},{2,6},{6,2},{3,7},{7,3},{8,12},{12,8},{9,1... | collective-permute-start | bytes 3145736 | tf_op jit(solution)/shard_map/ppermute | solution.py:620
  388.3 17.0 %collective-permute-start.6 = (f32[13824]{0:T(1024)S(1)}, f32[13824]{0:T(1024)S(1)}, u32[]{:S(2)}, u32[]{:S(2)}) collective-permute-start(f32[13824]{0:T(1024)S(1)} %pad_maximum_fusion), channel_id=1, source_target_pairs={{0,8},{4,20},{8,0},{12,28},{16,24},{20,4},{24,16},{28,12},{1,9},{5... | collective-permute-start | bytes 165896 | tf_op jit(solution)/shard_map/ppermute | solution.py:659
  403.9 7.0 %collective-permute-start.23 = (bf16[512,1024]{1,0:T(8,128)(2,1)S(1)}, bf16[512,1024]{1,0:T(8,128)(2,1)S(1)}, u32[]{:S(2)}, u32[]{:S(2)}) collective-permute-start(bf16[512,1024]{1,0:T(8,128)(2,1)S(1)} %get-tuple-element.57), channel_id=1, source_target_pairs={{0,4},{4,0},{1,5},{5,1},{2,6},{6,2},{3,7},{7,3},{8,12},{12,8},{9,1... | collective-permute-start | bytes 3145736 | tf_op jit(solution)/shard_map/ppermute | solution.py:620
  405.3 13.6 %copy-start.9 = (f32[512,1536]{1,0:T(8,128)}, f32[512,1536]{1,0:T(8,128)S(1)}, u32[]{:S(2)}) copy-start(f32[512,1536]{1,0:T(8,128)S(1)} %convert_dynamic-update-slice_fusion.2) | copy-start | bytes 9437188
  405.3 4.2 collective-permute-start.7
Sparse Core Ops, SparseCore 0:
  53.7 87.7 all-gather.1
  183.8 76.9 reduce-scatter.2
  263.6 76.7 reduce-scatter.4
where the time goes:
time: 434 us; the launch traced here: 426 us
  Pallas kernels  164 us (38%)
  matrix products  91.6 us (21%)
  other arithmetic  56.1 us (13%)
  waiting for transfers between devices  48 us (11%)
  local copies, waits for them, and re-layouts  30.2 us (7%)
  starting transfers between devices  18.6 us (4%)
  between operations  17.4 us (4%)
    dot_general x4, matrix products, contract_first(): lax.dot_general(left_mat, right_mat, (((0,), (0,)), ((), ())), preferred_...  42.6 us
    pallas_call x1, Pallas kernels, opening(): pl.pallas_call(functools.partial(opening_kernel, side=side, second=second...  39.6 us
    ppermute x14, waiting for transfers between devices, move(): return lax.ppermute(value, ('shard', 'ctx'), pairs)  38.5 us
    pallas_call x2, Pallas kernels, norm_grad(): pl.pallas_call(norm_grad_kernel, grid=(rows // step,), out_shape=(jax.Sha...  36.1 us
    pallas_call x10, Pallas kernels, block_sum(): pl.pallas_call(functools.partial(block_sum_kernel, count=len(received)),...  31.6 us
    pallas_call x2, Pallas kernels, pair_product(): pl.pallas_call(pair_product_kernel, grid=(rows // step,), out_shape=jax.S...  20 us
    pallas_call x1, Pallas kernels, attend(): pl.pallas_call(functools.partial(attend_kernel, block=block, count=count)...  19.3 us
    dot_general x1, matrix products, local(): pre_grad = jnp.dot(g_row, w_down, preferred_element_type=f32) * slope  17.5 us
  transfers between devices with their start and end apart: 27, of which 9 were waited for; matrix products, arithmetic and copies ran while one was open for 34% of the time, Pallas kernels for 25%

commit v1 on v0

--- a/solution.py
+++ b/solution.py
@@ -454,6 +454,38 @@
     )(jnp.asarray(index, jnp.int32).reshape(1), whole, *received, *after)
 
 
+def place_columns_kernel(rank_ref, *refs):
+    del rank_ref
+    for number, ref in enumerate(refs[:-1]):
+
+        @pl.when(pl.program_id(1) == number)
+        def _():
+            refs[-1][...] = ref[...].astype(refs[-1].dtype)
+
+
+def place_columns(parts, rank):
+    count = len(parts)
+    rows, columns = parts[0].shape
+    step = min(rows, 256)
+    tile = pl.BlockSpec((step, columns), lambda i, k, rank: (i, 0))
+    return pl.pallas_call(
+        place_columns_kernel,
+        grid_spec=pltpu.PrefetchScalarGridSpec(
+            num_scalar_prefetch=1,
+            grid=(rows // step, count),
+            in_specs=[tile] * count,
+            out_specs=pl.BlockSpec(
+                (step, columns), lambda i, k, rank: (i, lax.rem(rank[0] + k, count))
+            ),
+        ),
+        out_shape=jax.ShapeDtypeStruct((rows, columns * count), jnp.float32),
+        cost_estimate=pl.CostEstimate(
+            flops=0, bytes_accessed=6 * rows * columns * count, transcendentals=0
+        ),
+        name="place_columns",
+    )(jnp.asarray(rank, jnp.int32).reshape(1), *parts)
+
+
 def norm_grad_kernel(
     left_ref,
     right_ref,
@@ -658,7 +690,7 @@
                 pairs.append((shard * self.ranks + rank, target * self.ranks + rank))
         return lax.ppermute(value, ("shard", "ctx"), pairs)
 
-    def scatter_sum(self, partial, after):
+    def scatter_sum(self, partial, after, last=()):
         rows = partial.shape[0] // self.count
         sums, final = {}, []
         for b in list(range(1, self.second)) + [0]:
@@ -673,7 +705,7 @@
             else:
                 sums[b] = lax.dynamic_slice_in_dim(partial, self.index(0, b) * rows, rows)
         final = final + [self.move(sums[b], 0, b) for b in range(1, self.second)]
-        return block_sum(partial, self.index(0, 0), final, after, jnp.float32)
+        return block_sum(partial, self.index(0, 0), final, [*after, *last], partial.dtype)
 
     def full_sum(self, value):
         total = value
@@ -831,6 +863,7 @@
         total = block_sum(parts[0], 0, received, [], bf16)
         return total, lax.psum_scatter(total, "tp", scatter_dimension=1, tiled=True).astype(f32)
 
+    dense_local = contract_first(g_row, attn).astype(bf16)
     out_parts = {}
     for k in reversed(range(ctx_count)):
         out_parts[k] = pair_product(
@@ -838,7 +871,7 @@
             hidden,
             w_dense,
             w_wide,
-            [proj_grad_b] if k + 1 == ctx_count else [out_parts[k + 1]],
+            [proj_grad_b, dense_local] if k + 1 == ctx_count else [out_parts[k + 1]],
             k * tokens,
             tokens,
         )
@@ -847,15 +880,10 @@
     x_slice = lax.dynamic_slice_in_dim(x_mine, tp_rank * slice_width, slice_width, 1)
     output = x_slice.astype(f32) + summed_out + out_shift
 
-    def reduce_weight(grad, after):
-        mine = plane.scatter_sum(grad, after)
-        rows, columns = mine.shape
-        whole = jnp.zeros((rows, columns * ctx_count), f32)
-        for k in range(ctx_count):
-            part = mine if k == 0 else ring_shift(mine.astype(bf16), "ctx", ctx_count - k)
-            place = lax.rem(ctx_rank + k, ctx_count) * columns
-            whole = lax.dynamic_update_slice_in_dim(whole, part.astype(f32), place, 1)
-        return whole
+    def reduce_weight(grad, after, last=()):
+        mine = plane.scatter_sum(grad, after, last)
+        parts = [mine] + [ring_shift(mine, "ctx", ctx_count - k) for k in range(1, ctx_count)]
+        return place_columns(parts, ctx_rank)
 
     bias_grad = jnp.sum(g_row.astype(f32), axis=0)
 
@@ -878,19 +906,16 @@
             tokens,
         )
         norm_sums = norm_sums + sums
-    _, input_sum = reduce_partial(in_parts)
+    in_total, input_sum = reduce_partial(in_parts)
     g_slice = lax.dynamic_slice_in_dim(g_mine, tp_rank * slice_width, slice_width, 1)
     input_grad = g_slice.astype(f32) + input_sum
 
     down_local = contract_first(g_row, hidden).astype(bf16)
-    dense_local = contract_first(g_row, attn).astype(bf16)
     qkv_local = contract_first(acts_one, proj_grad_b).astype(bf16)
     up_local = contract_first(acts_two, pre_grad_b).astype(bf16)
-    late = [dense_local, qkv_local, up_local]
-    down_grad = reduce_weight(down_local, [in_parts[0]])
-    dense_grad = reduce_weight(dense_local, late)
-    qkv_grad = reduce_weight(qkv_local, late)
-    up_grad = reduce_weight(up_local, late)
+    late = [qkv_local, up_local]
+    down_grad = reduce_weight(down_local, [in_total])
+    dense_grad = reduce_weight(dense_local, [out_total])
 
     norm_sums = norm_sums.reshape(-1)
     column_sums = [up_bias_grad, qkv_bias_grad]
@@ -917,6 +942,8 @@
         norm_sums[k * width : (k + 1) * width] for k in range(4)
     ]
     reduced = plane.full_sum(jnp.concatenate(pieces))
+    qkv_grad = reduce_weight(qkv_local, late, [reduced])
+    up_grad = reduce_weight(up_local, late, [reduced])
     results, offset = [], 0
     for piece in pieces:
         own = piece.shape[0] // shard_count

time: 434 us -> 439 us (1.012)
  other arithmetic: 56.1 us -> 36.2 us
  Pallas kernels: 164 us -> 179 us
  waiting for transfers between devices: 48 us -> 61.9 us
  local copies, waits for them, and re-layouts: 30.2 us -> 25.4 us
    pallas_call x0 -> x4, Pallas kernels: none -> 16.4 us  [place_columns(): pl.pallas_call(place_columns_kernel, grid_spec=pltpu.PrefetchScalarGridSp...]
    ppermute x14, waiting for transfers between devices: 38.5 us -> 54.4 us  [move(): return lax.ppermute(value, ('shard', 'ctx'), pairs)]
    convert_element_type x4 -> x0, other arithmetic: 12.8 us -> none  [reduce_weight(): mine.astype(bf16)]
    dynamic_update_slice x4 -> x0, other arithmetic: 6.05 us -> none  [reduce_weight(): whole = lax.dynamic_update_slice_in_dim(whole, part.astype(f32), place, 1)]
    another operation x5 -> x3, local copies, waits for them, and re-layouts: 5.24 us -> 0.2 us
    all_gather x1, waiting for transfers between devices: 4.96 us -> 0.05 us  [local(): w_wide = lax.all_gather(wide_mine, 'shard', axis=0, tiled=True)]
  transfers between devices with their start and end apart: 27 -> 27, of which waited for: 9 -> 7; matrix products, arithmetic and copies ran while one was open for 34% -> 28% of each run, Pallas kernels for 25% -> 29%
where the time goes in v1:
time: 439 us; the launch traced here: 431 us
  Pallas kernels  179 us (41%)
  matrix products  91.1 us (21%)
  waiting for transfers between devices  61.9 us (14%)
  other arithmetic  36.2 us (8%)
  local copies, waits for them, and re-layouts  25.4 us (6%)
  starting transfers between devices  20.7 us (5%)
  between operations  17.3 us (4%)
    ppermute x14, waiting for transfers between devices, move(): return lax.ppermute(value, ('shard', 'ctx'), pairs)  54.4 us
    dot_general x4, matrix products, contract_first(): lax.dot_general(left_mat, right_mat, (((0,), (0,)), ((), ())), preferred_...  42.5 us
    pallas_call x1, Pallas kernels, opening(): pl.pallas_call(functools.partial(opening_kernel, side=side, second=second...  39.6 us
    pallas_call x2, Pallas kernels, norm_grad(): pl.pallas_call(norm_grad_kernel, grid=(rows // step,), out_shape=(jax.Sha...  35.1 us
    pallas_call x10, Pallas kernels, block_sum(): pl.pallas_call(functools.partial(block_sum_kernel, count=len(received)),...  31.1 us
    pallas_call x2, Pallas kernels, pair_product(): pl.pallas_call(pair_product_kernel, grid=(rows // step,), out_shape=jax.S...  20 us
    pallas_call x1, Pallas kernels, attend(): pl.pallas_call(functools.partial(attend_kernel, block=block, count=count)...  19 us
    dot_general x1, matrix products, local(): pre_grad = jnp.dot(g_row, w_down, preferred_element_type=f32) * slope  17.6 us
  transfers between devices with their start and end apart: 27, of which 7 were waited for; matrix products, arithmetic and copies ran while one was open for 28% of the time, Pallas kernels for 29%

profile of v1, /device:TPU:0, one launch (start us, length us, event | category | flops | bytes accessed | tf_op | source)
XLA Modules:
  0.0 431.1 jit_solution(9819428769410387922)
XLA Ops:
  12.0 1.9 concatenate.39.refs_0_
  14.0 39.6 %opening.1 = (bf16[64,512]{1,0:T(8,128)(2,1)}, bf16[2048,768]{1,0:T(8,128)(2,1)}, bf16[2048,256]{1,0:T(8,128)(2,1)}, bf16[2048,2048]{1,0:T(8,128)(2,1)}, bf16[20...) custom-call(bf16[16,512]{1,0:T(8,128)(2,1)} %concatenate.39.refs_0_, bf16[512,1536]{1,0:T(8,128)(2,1)} %refs_1_.1, ...), custom_call_target="tpu_custom_call" | custom-call | tf_op jit(solution)/shard_map/opening/pallas_call | solution.py:392
  57.8 1.3 copy.36.seg_col_ref
  59.4 3.7 multiply_sine_fusion
  63.1 1.0 concatenate.44.low_ref
  65.7 4.7 %convert_reduce_fusion = f32[2048]{0:T(1024)S(1)} fusion(bf16[2048,2048]{1,0:T(8,128)(2,1)} %get-tuple-element.30.x_ref), kind=kLoop, calls=%fused_computation.1 | loop fusion | flops 8386560 | bytes 8396800 | tf_op jit(solution)/shard_map/reduce_sum | solution.py:810
  70.5 5.8 %fusion.8 = f32[2048]{0:T(1024)S(1)} fusion(bf16[2048,2048]{1,0:T(8,128)(2,1)} %get-tuple-element.30.x_ref, f32[2048]{0:T(1024)S(1)} %broadcast_multiply_fusion), kind=kLoop, calls=%fused_computation.10 | loop fusion | flops 16775168 | bytes 8404992 | tf_op jit(solution)/shard_map/reduce_sum | solution.py:811
  76.3 1.3 maximum_maximum_fusion.cos_ref
  77.6 1.3 maximum_maximum_fusion.1.high_ref
  79.0 3.9 fusion.5
  82.9 8.5 %broadcast_add_fusion.proj_ref = f32[2048,768]{1,0:T(8,128)} fusion(f32[768]{0:T(1024)S(1)} %dynamic-slice.10, bf16[2048,2048]{1,0:T(8,128)(2,1)S(1)} %fusion.5, bf16[2048,768]{1,0:T(8,128)(2,1)S(1)} %copy-done.6), kind=kOutput, calls=%fused_computation.26 | convolution fusion | flops 6444023808 | bytes 17828864 | tf_op jit(solution)/shard_map/dot_general | solution.py:816
  91.4 19.0 %attend.1 = (bf16[2048,256]{1,0:T(8,128)(2,1)}, bf16[2048,256]{1,0:T(8,128)(2,1)}, bf16[2048,256]{1,0:T(8,128)(2,1)}, bf16[2048,256]{1,0:T(8,128)(2,1)}, f32[2048,1]{1,0:T(8,128)}) custom-call(s32[4]{0:T(128)} %pad_add_fusion.2.order_ref, s32[2,4]{1,0:T(2,128)} %pad_add_fusion.1.bounds_ref, f32[2048,768]{1,0:T(8,128)} %broadcast_add_fusion.proj_ref, ...), custom_call_target="tpu_custom_call" | custom-call | flops 2147483648 | bytes 8388608 | tf_op jit(solution)/shard_map/attend/pallas_call | solution.py:599
  110.4 6.7 %convolution_convert_fusion.4.grad_ref = bf16[2048,256]{1,0:T(8,128)(2,1)} fusion(bf16[2048,2048]{1,0:T(8,128)(2,1)} %get-tuple-element.39, bf16[2048,256]{1,0:T(8,128)(2,1)S(1)} %copy-done.8), kind=kOutput, calls=%fused_computation.28 | convolution fusion | flops 2148007936 | bytes 10485760 | tf_op jit(solution)/shard_map/dot_general | solution.py:833
  117.1 17.4 %attend_grad.1 = (bf16[2048,768]{1,0:T(8,128)(2,1)}, f32[1,768]{1,0:T(1,128)}) custom-call(s32[4]{0:T(128)} %pad_add_fusion.2.order_ref, s32[2,4]{1,0:T(2,128)} %pad_add_fusion.1.bounds_ref, bf16[2048,256]{1,0:T(8,128)(2,1)} %get-tuple-element.36.query_ref, bf16[2048,256]{1,0:T(8,128)(2,1)} %get-tuple-element.37.key_ref, ...), custom_call_target="tpu_custom_call" | custom-call | flops 5368709120 | bytes 8388608 | tf_op jit(solution)/shard_map/attend_grad/pallas_call | solution.py:628
  134.6 6.9 %convolution_convert_fusion.3.refs_1_.whole_ref = bf16[2048,256]{1,0:T(8,128)(2,1)} fusion(bf16[2048,2048]{1,0:T(8,128)(2,1)} %get-tuple-element.39, bf16[2048,256]{1,0:T(8,128)(2,1)S(1)} %copy-done.9), kind=kOutput, calls=%fused_computation.27 | convolution fusion | flops 2148007936 | bytes 10485760 | tf_op jit(solution)/shard_map/dot_general | solution.py:56
  141.5 15.8 %multiply_convert_fusion = (bf16[2048,1024]{1,0:T(8,128)(2,1)}, f32[2048,1024]{1,0:T(8,128)}) fusion(f32[1024]{0:T(1024)S(1)} %dynamic-slice.11, bf16[2048,2048]{1,0:T(8,128)(2,1)} %all-gather.2.cloned.1.call-done.right_weight, bf16[2048,2048]{1,0:T(8,128)(2,1)} %get-tuple-element.30.x_ref, f32[2048]{0:T(1024)S(1)} %bitcast.86, f32[2048]{0:T(1024)S(1)} %bitcast.88, ...), kind=kOutput, calls=%fused_computation.18 | convolution fusion | flops 8627683328 | bytes 25202688 | tf_op jit(solution)/shard_map/dot_general | solution.py:856
  157.3 10.0 %pair_product.2.refs_0_ = bf16[1024,2048]{1,0:T(8,128)(2,1)} custom-call(bf16[2048,256]{1,0:T(8,128)(2,1)} %get-tuple-element.33.attn_ref.left_ref, bf16[2048,1024]{1,0:T(8,128)(2,1)} %get-tuple-element.91.right_ref, bf16[2048,256]{1,0:T(8,128)(2,1)} %get-tuple-element.35.left_weight, bf16[2048,2048]{1,0:T(8,128)(2,1)} %all-gather.2.cloned.1.call-done.right_weight, ...), custom_call_target="tpu_custom_call" | custom-call | flops 5368709120 | bytes 6815744 | tf_op jit(solution)/shard_map/pair_product/pallas_call | solution.py:543
  167.3 10.0 %pair_product.3.whole_ref = bf16[1024,2048]{1,0:T(8,128)(2,1)} custom-call(bf16[2048,256]{1,0:T(8,128)(2,1)} %get-tuple-element.33.attn_ref.left_ref, bf16[2048,1024]{1,0:T(8,128)(2,1)} %get-tuple-element.91.right_ref, bf16[2048,256]{1,0:T(8,128)(2,1)} %get-tuple-element.35.left_weight, bf16[2048,2048]{1,0:T(8,128)(2,1)} %all-gather.2.cloned.1.call-done.right_weight, ...), custom_call_target="tpu_custom_call" | custom-call | flops 5368709120 | bytes 6815744 | tf_op jit(solution)/shard_map/pair_product/pallas_call | solution.py:543
  177.3 6.0 %block_sum.10.after_ref.refs_1_.refs_2_ = bf16[1024,2048]{1,0:T(8,128)(2,1)} custom-call(s32[1]{0:T(128)} %constant.109.clone.1.index_ref, bf16[1024,2048]{1,0:T(8,128)(2,1)} %pair_product.3.whole_ref, bf16[1024,2048]{1,0:T(8,128)(2,1)} %collective-permute-done.refs_0_), custom_call_target="tpu_custom_call" | custom-call | flops 2097152 | bytes 12582912 | tf_op jit(solution)/shard_map/block_sum/pallas_call | solution.py:439
  184.6 17.6 %fusion.23 = (f32[1024]{0:T(1024)S(1)}, bf16[2048,1024]{1,0:T(8,128)(2,1)}) fusion(f32[2048,1024]{1,0:T(8,128)} %get-tuple-element.92, f32[1024]{0:T(1024)S(1)} %dynamic-slice.11, bf16[2048,2048]{1,0:T(8,128)(2,1)} %get-tuple-element.39, bf16[2048,2048]{1,0:T(8,128)(2,1)} %all-gather.2.cloned.1.call-done.right_weight), kind=kOutput, calls=%fused_computation.82 | convolution fusion | flops 8615099392 | bytes 25174016 | tf_op jit(solution)/shard_map/dot_general | solution.py:890
  202.2 17.7 %norm_grad.2 = (bf16[1024,2048]{1,0:T(8,128)(2,1)}, f32[4,2048]{1,0:T(4,128)}) custom-call(bf16[2048,768]{1,0:T(8,128)(2,1)} %get-tuple-element.41.refs_0_.left_ref, bf16[2048,1024]{1,0:T(8,128)(2,1)} %get-tuple-element.50.right_ref, bf16[2048,2048]{1,0:T(8,128)(2,1)} %get-tuple-element.30.x_ref, bf16[2048,768]{1,0:T(8,128)(2,1)} %get-tuple-element.32.left_weight, ...), custom_call_target="tpu_custom_call" | custom-call | flops 7516192768 | bytes 12058624 | tf_op jit(solution)/shard_map/norm_grad/pallas_call | solution.py:567
  220.7 9.5 %convolution_convert_fusion.2.whole_ref.refs_1_.refs_2_ = bf16[2048,768]{1,0:T(8,128)(2,1)S(1)} fusion(bf16[2048,2048]{1,0:T(8,128)(2,1)} %copy-done.7, bf16[2048,768]{1,0:T(8,128)(2,1)S(1)} %copy-done.2), kind=kOutput, calls=%fused_computation.25 | convolution fusion | flops 6444023808 | bytes 14680064 | tf_op jit(solution)/shard_map/dot_general | solution.py:56
  230.2 1.4 constant_dynamic-slice_fusion.6
  231.6 4.9 %convert_reduce_fusion.1 = f32[2048]{0:T(1024)S(1)} fusion(bf16[2048,2048]{1,0:T(8,128)(2,1)} %get-tuple-element.39), kind=kLoop, calls=%fused_computation.11 | loop fusion | flops 8386560 | bytes 8396800 | tf_op jit(solution)/shard_map/reduce_sum | solution.py:888
  236.5 17.5 %norm_grad.3 = (bf16[1024,2048]{1,0:T(8,128)(2,1)}, f32[4,2048]{1,0:T(4,128)}) custom-call(bf16[2048,768]{1,0:T(8,128)(2,1)} %get-tuple-element.41.refs_0_.left_ref, bf16[2048,1024]{1,0:T(8,128)(2,1)} %get-tuple-element.50.right_ref, bf16[2048,2048]{1,0:T(8,128)(2,1)} %get-tuple-element.30.x_ref, bf16[2048,768]{1,0:T(8,128)(2,1)} %get-tuple-element.32.left_weight, ...), custom_call_target="tpu_custom_call" | custom-call | flops 7516192768 | bytes 12058624 | tf_op jit(solution)/shard_map/norm_grad/pallas_call | solution.py:567
  253.9 6.1 %block_sum.11.refs_1_.refs_2_ = bf16[1024,2048]{1,0:T(8,128)(2,1)} custom-call(s32[1]{0:T(128)} %constant.109.clone.1.index_ref, bf16[1024,2048]{1,0:T(8,128)(2,1)} %get-tuple-element.43.whole_ref, bf16[1024,2048]{1,0:T(8,128)(2,1)} %collective-permute-done.1.refs_0_), custom_call_target="tpu_custom_call" | custom-call | flops 2097152 | bytes 12582912 | tf_op jit(solution)/shard_map/block_sum/pallas_call | solution.py:439
  260.1 12.8 %convolution_convert_fusion.whole_ref = bf16[2048,1024]{1,0:T(8,128)(2,1)S(1)} fusion(bf16[2048,2048]{1,0:T(8,128)(2,1)} %get-tuple-element.39, bf16[2048,1024]{1,0:T(8,128)(2,1)} %get-tuple-element.91.right_ref), kind=kOutput, calls=%fused_computation.23 | convolution fusion | flops 8592031744 | bytes 16777216 | tf_op jit(solution)/shard_map/dot_general | solution.py:56
  272.9 1.3 constant_dynamic-slice_fusion
  274.2 1.0 copy-done.3
  275.2 1.5 collective-permute-start.21
  276.7 13.3 %convolution_convert_fusion.1.refs_2_.refs_3_.whole_ref = bf16[2048,1024]{1,0:T(8,128)(2,1)S(1)} fusion(bf16[2048,1024]{1,0:T(8,128)(2,1)S(1)} %copy-done.4, bf16[2048,2048]{1,0:T(8,128)(2,1)} %get-tuple-element.30.x_ref, f32[2048]{0:T(1024)S(1)} %bitcast.87, f32[2048]{0:T(1024)S(1)} %bitcast.89, f32[2048]{0:T(1024)S(1)} %add_rsqrt_fusion, ...), kind=kOutput, calls=%fused_computation.24 | convolution fusion | flops 8617197568 | bytes 16809984 | tf_op jit(solution)/shard_map/dot_general | solution.py:56
  290.2 1.9 copy-done
  292.1 1.1 constant_dynamic-slice_fusion.2
  293.7 1.5 collective-permute-start.16
  295.4 3.4 collective-permute-start.5
  298.9 2.3 collective-permute-done.5
  302.1 5.1 %collective-permute-done.4 = f32[8192]{0:T(1024)S(1)} collective-permute-done((f32[8192]{0:T(1024)S(1)}, f32[8192]{0:T(1024)S(1)}, u32[]{:S(2)}, u32[]{:S(2)}) %collective-permute-start.4) | collective-permute-done | bytes 32800 | tf_op jit(solution)/shard_map/ppermute | solution.py:652
  307.1 1.3 collective-permute-start.9
  309.3 2.4 block_sum.16
  311.7 1.4 collective-permute-start.18
  313.1 1.4 collective-permute-start.20
  314.5 2.4 block_sum.18
  316.9 22.8 %collective-permute-done.6 = f32[13824]{0:T(1024)S(1)} collective-permute-done((f32[13824]{0:T(1024)S(1)}, f32[13824]{0:T(1024)S(1)}, u32[]{:S(2)}, u32[]{:S(2)}) %collective-permute-start.6) | collective-permute-done | bytes 55328 | tf_op jit(solution)/shard_map/ppermute | solution.py:691
  340.4 1.5 collective-permute-start.7
  341.8 2.2 block_sum.12
  344.6 22.6 %collective-permute-done.7 = f32[13824]{0:T(1024)S(1)} collective-permute-done((f32[13824]{0:T(1024)S(1)}, f32[13824]{0:T(1024)S(1)}, u32[]{:S(2)}, u32[]{:S(2)}) %collective-permute-start.7) | collective-permute-done | bytes 55328 | tf_op jit(solution)/shard_map/ppermute | solution.py:691
  368.5 2.8 block_sum.17.refs_0_
  371.3 2.9 block_sum.19.refs_0_
  375.4 1.3 collective-permute-start.13
  376.7 3.9 collective-permute-done.10.refs_1_
  380.6 2.5 block_sum.13.refs_0_
  383.1 1.8 block_sum.14
  385.0 2.0 collective-permute-start.14
  387.0 3.8 collective-permute-done.12.refs_0_
  390.7 1.2 collective-permute-done.14.refs_1_
  392.0 1.9 block_sum.15.refs_0_
  396.4 1.4 fusion.24
  398.5 3.0 place_columns.5
  402.4 4.1 place_columns.4
  406.5 1.0 copy-done.10
  407.4 4.6 %place_columns.6 = f32[512,2048]{1,0:T(8,128)} custom-call(s32[1]{0:T(128)} %bitcast.21.rank_ref, bf16[512,1024]{1,0:T(8,128)(2,1)} %block_sum.17.refs_0_, bf16[512,1024]{1,0:T(8,128)(2,1)} %copy-done.10), custom_call_target="tpu_custom_call" | custom-call | bytes 6291456 | tf_op jit(solution)/shard_map/place_columns/pallas_call | solution.py:471
  413.1 4.6 %place_columns.7 = f32[512,2048]{1,0:T(8,128)} custom-call(s32[1]{0:T(128)} %bitcast.21.rank_ref, bf16[512,1024]{1,0:T(8,128)(2,1)} %block_sum.19.refs_0_, bf16[512,1024]{1,0:T(8,128)(2,1)} %copy-done.11), custom_call_target="tpu_custom_call" | custom-call | bytes 6291456 | tf_op jit(solution)/shard_map/place_columns/pallas_call | solution.py:471
  417.7 3.2 add_add_fusion
  420.9 3.2 convert_add_fusion
  (155 shorter events, 21.8 us)
Async XLA Ops:
  7.2 134.3 %all-gather.2.cloned.1.call-start = ((), (), s32[]{:S(2)}) async-start(), calls=%async_computation.2 | async-start | bytes 10485760 | tf_op jit(solution)/shard_map/all_gather | solution.py:771
  14.0 39.7 %copy-start.22 = (s32[4]{0:T(128)S(1)}, s32[4]{0:T(128)}, u32[]{:S(2)}) copy-start(s32[4]{0:T(128)} %param.19) | copy-start | bytes 52
  14.0 43.1 %copy-start.17 = (s32[1,2048]{1,0:T(1,128)S(1)}, s32[1,2048]{1,0:T(1,128)}, u32[]{:S(2)}) copy-start(s32[1,2048]{1,0:T(1,128)} %param.18) | copy-start | bytes 24580
  53.5 10.7 %copy-start.18 = (bf16[64,512]{1,0:T(8,128)(2,1)S(1)}, bf16[64,512]{1,0:T(8,128)(2,1)}, u32[]{:S(2)}) copy-start(bf16[64,512]{1,0:T(8,128)(2,1)} %get-tuple-element.31) | copy-start | bytes 196612
  53.6 364.1 %reduce-scatter.3.cloned.1.call-start = ((), (), s32[]{:S(2)}) async-start(), calls=%async_computation.3 | async-start | bytes 5242880 | tf_op jit(solution)/shard_map/reduce_scatter | solution.py:864
  57.7 18.6 %copy-start.16 = (s32[2048]{0:T(1024)}, s32[2048]{0:T(1024)S(1)}, u32[]{:S(2)}) copy-start(s32[2048]{0:T(1024)S(1)} %pad_add_fusion) | copy-start | bytes 24580
  65.7 13.2 %slice-start = ((s8[8388608]{0:T(1024)(128)(4,1)}), s8[4194304]{0:T(1024)(128)(4,1)S(1)}, s32[]{:S(2)}) async-start(s8[8388608]{0:T(1024)(128)(4,1)} %bitcast.62), calls=%async_computation.5 | async-start | bytes 8388608
  70.4 8.5 %slice-start.1 = ((s8[8388608]{0:T(1024)(128)(4,1)}), s8[4194304]{0:T(1024)(128)(4,1)S(1)}, s32[]{:S(2)}) async-start(s8[8388608]{0:T(1024)(128)(4,1)} %bitcast.62), calls=%async_computation.6 | async-start | bytes 8388608
  78.9 3.9 copy-start.6
  82.9 8.5 %copy-start.7 = (bf16[2048,2048]{1,0:T(8,128)(2,1)}, bf16[2048,2048]{1,0:T(8,128)(2,1)S(1)}, u32[]{:S(2)}) copy-start(bf16[2048,2048]{1,0:T(8,128)(2,1)S(1)} %fusion.5) | copy-start | bytes 25165828
  91.4 19.0 %copy-start.8 = (bf16[2048,256]{1,0:T(8,128)(2,1)S(1)}, bf16[2048,256]{1,0:T(8,128)(2,1)}, u32[]{:S(2)}) copy-start(bf16[2048,256]{1,0:T(8,128)(2,1)} %get-tuple-element.35.left_weight) | copy-start | bytes 3145732
  117.1 17.4 %copy-start.9 = (bf16[2048,256]{1,0:T(8,128)(2,1)S(1)}, bf16[2048,256]{1,0:T(8,128)(2,1)}, u32[]{:S(2)}) copy-start(bf16[2048,256]{1,0:T(8,128)(2,1)} %get-tuple-element.33.attn_ref.left_ref) | copy-start | bytes 3145732
  167.3 10.0 %collective-permute-start = (bf16[1024,2048]{1,0:T(8,128)(2,1)}, bf16[1024,2048]{1,0:T(8,128)(2,1)}, u32[]{:S(2)}, u32[]{:S(2)}) collective-permute-start(bf16[1024,2048]{1,0:T(8,128)(2,1)} %pair_product.2.refs_0_), channel_id=1, source_target_pairs={{0,4},{4,0},{1,5},{5,1},{2,6},{6,2},{3,7},{7,3},{8,12},{12,8},{9,1... | collective-permute-start | bytes 12582920 | tf_op jit(solution)/shard_map/ppermute | solution.py:652
  183.3 237.6 %reduce-scatter.5.cloned.1.call-start = ((), (), s32[]{:S(2)}) async-start(), calls=%async_computation.4 | async-start | bytes 5242880 | tf_op jit(solution)/shard_map/reduce_scatter | solution.py:864
  202.2 18.2 %copy-start.21 = (f32[1,768]{1,0:T(1,128)S(1)}, f32[1,768]{1,0:T(1,128)}, u32[]{:S(2)}) copy-start(f32[1,768]{1,0:T(1,128)} %get-tuple-element.46) | copy-start | bytes 9220
  202.2 18.5 %copy-start.2 = (bf16[2048,768]{1,0:T(8,128)(2,1)S(1)}, bf16[2048,768]{1,0:T(8,128)(2,1)}, u32[]{:S(2)}) copy-start(bf16[2048,768]{1,0:T(8,128)(2,1)} %get-tuple-element.41.refs_0_.left_ref) | copy-start | bytes 9437188
  219.8 34.1 %collective-permute-start.1 = (bf16[1024,2048]{1,0:T(8,128)(2,1)}, bf16[1024,2048]{1,0:T(8,128)(2,1)}, u32[]{:S(2)}, u32[]{:S(2)}) collective-permute-start(bf16[1024,2048]{1,0:T(8,128)(2,1)} %get-tuple-element.42.after_ref), channel_id=1, source_target_pairs={{0,4},{4,0},{1,5},{5,1},{2,6},{6,2},{3,7},{7,3},{8,12},{12,8},{9,1... | collective-permute-start | bytes 12582920 | tf_op jit(solution)/shard_map/ppermute | solution.py:652
  230.2 23.8 %copy-start.1 = (bf16[2048,768]{1,0:T(8,128)(2,1)}, bf16[2048,768]{1,0:T(8,128)(2,1)S(1)}, u32[]{:S(2)}) copy-start(bf16[2048,768]{1,0:T(8,128)(2,1)S(1)} %convolution_convert_fusion.2.whole_ref.refs_1_.refs_2_) | copy-start | bytes 9437188
  260.1 16.7 %copy-start.4 = (bf16[2048,1024]{1,0:T(8,128)(2,1)S(1)}, bf16[2048,1024]{1,0:T(8,128)(2,1)}, u32[]{:S(2)}) copy-start(bf16[2048,1024]{1,0:T(8,128)(2,1)} %get-tuple-element.50.right_ref) | copy-start | bytes 12582916
  272.9 2.3 copy-start.3
  275.2 14.8 %copy-start.19 = (f32[4,2048]{1,0:T(4,128)S(1)}, f32[4,2048]{1,0:T(4,128)}, u32[]{:S(2)}) copy-start(f32[4,2048]{1,0:T(4,128)} %get-tuple-element.44) | copy-start | bytes 98308
  275.2 14.9 %copy-start.20 = (f32[4,2048]{1,0:T(4,128)S(1)}, f32[4,2048]{1,0:T(4,128)}, u32[]{:S(2)}) copy-start(f32[4,2048]{1,0:T(4,128)} %get-tuple-element.45) | copy-start | bytes 98308
  275.2 37.9 %collective-permute-start.21 = (bf16[512,1024]{1,0:T(8,128)(2,1)}, bf16[512,1024]{1,0:T(8,128)(2,1)}, u32[]{:S(2)}, u32[]{:S(2)}) collective-permute-start(bf16[512,1024]{1,0:T(8,128)(2,1)} %get-tuple-element.51), channel_id=1, source_target_pairs={{0,8},{4,20},{8,0},{12,28},{16,24},{20,4},{24,16},{28,12},{1,9},{5... | collective-permute-start | bytes 3145736 | tf_op jit(solution)/shard_map/ppermute | solution.py:691
  290.0 2.0 copy-start
  290.1 5.3 %collective-permute-start.2 = (f32[9984]{0:T(1024)S(1)}, f32[9984]{0:T(1024)S(1)}, u32[]{:S(2)}, u32[]{:S(2)}) collective-permute-start(f32[9984]{0:T(1024)S(1)} %pad_maximum_fusion.1), channel_id=1, source_target_pairs={{0,4},{4,0},{1,5},{5,1},{2,6},{6,2},{3,7},{7,3},{8,12},{12,8},{9,1... | collective-permute-start | bytes 119816 | tf_op jit(solution)/shard_map/ppermute | solution.py:652
  293.2 16.1 %collective-permute-start.17 = (bf16[512,1024]{1,0:T(8,128)(2,1)}, bf16[512,1024]{1,0:T(8,128)(2,1)}, u32[]{:S(2)}, u32[]{:S(2)}) collective-permute-start(bf16[512,1024]{1,0:T(8,128)(2,1)} %get-tuple-element.53), channel_id=1, source_target_pairs={{0,8},{4,20},{8,0},{12,28},{16,24},{20,4},{24,16},{28,12},{1,9},{5... | collective-permute-start | bytes 3145736 | tf_op jit(solution)/shard_map/ppermute | solution.py:691
  293.7 50.4 %collective-permute-start.16 = (bf16[512,1024]{1,0:T(8,128)(2,1)S(1)}, bf16[512,1024]{1,0:T(8,128)(2,1)S(1)}, u32[]{:S(2)}, u32[]{:S(2)}) collective-permute-start(bf16[512,1024]{1,0:T(8,128)(2,1)S(1)} %get-tuple-element.54), channel_id=1, source_target_pairs={{0,8},{4,20},{8,0},{12,28},{16,24},{20,4},{24,16},{28,12},{1,9},{5... | collective-permute-start | bytes 3145736 | tf_op jit(solution)/shard_map/ppermute | solution.py:691
  295.4 5.7 %collective-permute-start.5 = (f32[8192]{0:T(1024)S(1)}, f32[8192]{0:T(1024)S(1)}, u32[]{:S(2)}, u32[]{:S(2)}) collective-permute-start(f32[8192]{0:T(1024)S(1)} %slice_add_fusion), channel_id=1, source_target_pairs={{0,3},{1,0},{2,1},{3,2},{4,7},{5,4},{6,5},{7,6},{8,11},{9,8},{10,9... | collective-permute-start | bytes 98312 | tf_op jit(solution)/shard_map/ppermute | solution.py:652
  298.8 8.4 %collective-permute-start.4 = (f32[8192]{0:T(1024)S(1)}, f32[8192]{0:T(1024)S(1)}, u32[]{:S(2)}, u32[]{:S(2)}) collective-permute-start(f32[8192]{0:T(1024)S(1)} %slice_add_fusion), channel_id=1, source_target_pairs={{0,2},{1,3},{2,0},{3,1},{4,6},{5,7},{6,4},{7,5},{8,10},{9,11},{10,... | collective-permute-start | bytes 98312 | tf_op jit(solution)/shard_map/ppermute | solution.py:652
  301.1 7.3 %collective-permute-start.3 = (f32[8192]{0:T(1024)S(1)}, f32[8192]{0:T(1024)S(1)}, u32[]{:S(2)}, u32[]{:S(2)}) collective-permute-start(f32[8192]{0:T(1024)S(1)} %slice_add_fusion), channel_id=1, source_target_pairs={{0,1},{1,2},{2,3},{3,0},{4,5},{5,6},{6,7},{7,4},{8,9},{9,10},{10,1... | collective-permute-start | bytes 98312 | tf_op jit(solution)/shard_map/ppermute | solution.py:652
  307.1 33.2 %collective-permute-start.9 = (bf16[512,768]{1,0:T(8,128)(2,1)}, bf16[512,768]{1,0:T(8,128)(2,1)}, u32[]{:S(2)}, u32[]{:S(2)}) collective-permute-start(bf16[512,768]{1,0:T(8,128)(2,1)} %get-tuple-element.55), channel_id=1, source_target_pairs={{0,8},{4,20},{8,0},{12,28},{16,24},{20,4},{24,16},{28,12},{1,9},{5... | collective-permute-start | bytes 2359304 | tf_op jit(solution)/shard_map/ppermute | solution.py:691
  308.5 31.3 %collective-permute-start.6 = (f32[13824]{0:T(1024)S(1)}, f32[13824]{0:T(1024)S(1)}, u32[]{:S(2)}, u32[]{:S(2)}) collective-permute-start(f32[13824]{0:T(1024)S(1)} %pad_maximum_fusion), channel_id=1, source_target_pairs={{0,8},{4,20},{8,0},{12,28},{16,24},{20,4},{24,16},{28,12},{1,9},{5... | collective-permute-start | bytes 165896 | tf_op jit(solution)/shard_map/ppermute | solution.py:691
  311.7 56.8 %collective-permute-start.18 = (bf16[512,1024]{1,0:T(8,128)(2,1)}, bf16[512,1024]{1,0:T(8,128)(2,1)}, u32[]{:S(2)}, u32[]{:S(2)}) collective-permute-start(bf16[512,1024]{1,0:T(8,128)(2,1)} %block_sum.16), channel_id=1, source_target_pairs={{0,16},{4,12},{8,24},{12,4},{16,0},{20,28},{24,8},{28,20},{1,17},{... | collective-permute-start | bytes 3145736 | tf_op jit(solution)/shard_map/ppermute | solution.py:691
  313.1 58.2 %collective-permute-start.20 = (bf16[512,1024]{1,0:T(8,128)(2,1)S(1)}, bf16[512,1024]{1,0:T(8,128)(2,1)}, u32[]{:S(2)}, u32[]{:S(2)}) collective-permute-start(bf16[512,1024]{1,0:T(8,128)(2,1)S(1)} %get-tuple-element.52), channel_id=1, source_target_pairs={{0,8},{4,20},{8,0},{12,28},{16,24},{20,4},{24,16},{28,12},{1,9},{5... | collective-permute-start | bytes 3145736 | tf_op jit(solution)/shard_map/ppermute | solution.py:691
  339.7 31.6 %collective-permute-start.22 = (bf16[512,1024]{1,0:T(8,128)(2,1)}, bf16[512,1024]{1,0:T(8,128)(2,1)}, u32[]{:S(2)}, u32[]{:S(2)}) collective-permute-start(bf16[512,1024]{1,0:T(8,128)(2,1)} %block_sum.18), channel_id=1, source_target_pairs={{0,16},{4,12},{8,24},{12,4},{16,0},{20,28},{24,8},{28,20},{1,17},{... | collective-permute-start | bytes 3145736 | tf_op jit(solution)/shard_map/ppermute | solution.py:691
  340.4 26.8 %collective-permute-start.7 = (f32[13824]{0:T(1024)S(1)}, f32[13824]{0:T(1024)S(1)}, u32[]{:S(2)}, u32[]{:S(2)}) collective-permute-start(f32[13824]{0:T(1024)S(1)} %fusion.20), channel_id=1, source_target_pairs={{0,16},{4,12},{8,24},{12,4},{16,0},{20,28},{24,8},{28,20},{1,17},{... | collective-permute-start | bytes 165896 | tf_op jit(solution)/shard_map/ppermute | solution.py:691
  344.1 24.4 %copy-start.12 = (bf16[512,1024]{1,0:T(8,128)(2,1)}, bf16[512,1024]{1,0:T(8,128)(2,1)S(1)}, u32[]{:S(2)}) copy-start(bf16[512,1024]{1,0:T(8,128)(2,1)S(1)} %collective-permute-done.16.refs_0_) | copy-start | bytes 3145732
  344.1 32.7 %collective-permute-start.8 = (bf16[512,768]{1,0:T(8,128)(2,1)}, bf16[512,768]{1,0:T(8,128)(2,1)}, u32[]{:S(2)}, u32[]{:S(2)}) collective-permute-start(bf16[512,768]{1,0:T(8,128)(2,1)} %get-tuple-element.56), channel_id=1, source_target_pairs={{0,8},{4,20},{8,0},{12,28},{16,24},{20,4},{24,16},{28,12},{1,9},{5... | collective-permute-start | bytes 2359304 | tf_op jit(solution)/shard_map/ppermute | solution.py:691
  367.2 13.4 %collective-permute-start.10 = (bf16[512,768]{1,0:T(8,128)(2,1)}, bf16[512,768]{1,0:T(8,128)(2,1)}, u32[]{:S(2)}, u32[]{:S(2)}) collective-permute-start(bf16[512,768]{1,0:T(8,128)(2,1)} %block_sum.12), channel_id=1, source_target_pairs={{0,16},{4,12},{8,24},{12,4},{16,0},{20,28},{24,8},{28,20},{1,17},{... | collective-permute-start | bytes 2359304 | tf_op jit(solution)/shard_map/ppermute | solution.py:691
  371.3 3.3 copy-start.5
  371.3 35.2 %collective-permute-start.19 = (bf16[512,1024]{1,0:T(8,128)(2,1)}, bf16[512,1024]{1,0:T(8,128)(2,1)S(1)}, u32[]{:S(2)}, u32[]{:S(2)}) collective-permute-start(bf16[512,1024]{1,0:T(8,128)(2,1)} %block_sum.17.refs_0_), channel_id=1, source_target_pairs={{0,4},{4,0},{1,5},{5,1},{2,6},{6,2},{3,7},{7,3},{8,12},{12,8},{9,1... | collective-permute-start | bytes 3145736 | tf_op jit(solution)/shard_map/ppermute | solution.py:652
  374.2 37.9 %collective-permute-start.23 = (bf16[512,1024]{1,0:T(8,128)(2,1)}, bf16[512,1024]{1,0:T(8,128)(2,1)S(1)}, u32[]{:S(2)}, u32[]{:S(2)}) collective-permute-start(bf16[512,1024]{1,0:T(8,128)(2,1)} %block_sum.19.refs_0_), channel_id=1, source_target_pairs={{0,4},{4,0},{1,5},{5,1},{2,6},{6,2},{3,7},{7,3},{8,12},{12,8},{9,1... | collective-permute-start | bytes 3145736 | tf_op jit(solution)/shard_map/ppermute | solution.py:652
  375.4 7.8 %collective-permute-start.13 = (bf16[512,256]{1,0:T(8,128)(2,1)}, bf16[512,256]{1,0:T(8,128)(2,1)}, u32[]{:S(2)}, u32[]{:S(2)}) collective-permute-start(bf16[512,256]{1,0:T(8,128)(2,1)} %get-tuple-element.57), channel_id=1, source_target_pairs={{0,8},{4,20},{8,0},{12,28},{16,24},{20,4},{24,16},{28,12},{1,9},{5... | collective-permute-start | bytes 786440 | tf_op jit(solution)/shard_map/ppermute | solution.py:691
  383.1 18.4 %collective-permute-start.11 = (bf16[512,768]{1,0:T(8,128)(2,1)}, bf16[512,768]{1,0:T(8,128)(2,1)S(1)}, u32[]{:S(2)}, u32[]{:S(2)}) collective-permute-start(bf16[512,768]{1,0:T(8,128)(2,1)} %block_sum.13.refs_0_), channel_id=1, source_target_pairs={{0,4},{4,0},{1,5},{5,1},{2,6},{6,2},{3,7},{7,3},{8,12},{12,8},{9,1... | collective-permute-start | bytes 2359304 | tf_op jit(solution)/shard_map/ppermute | solution.py:652
  383.1 7.6 %collective-permute-start.12 = (bf16[512,256]{1,0:T(8,128)(2,1)S(1)}, bf16[512,256]{1,0:T(8,128)(2,1)S(1)}, u32[]{:S(2)}, u32[]{:S(2)}) collective-permute-start(bf16[512,256]{1,0:T(8,128)(2,1)S(1)} %get-tuple-element.58), channel_id=1, source_target_pairs={{0,8},{4,20},{8,0},{12,28},{16,24},{20,4},{24,16},{28,12},{1,9},{5... | collective-permute-start | bytes 786440 | tf_op jit(solution)/shard_map/ppermute | solution.py:691
  385.0 7.0 %collective-permute-start.14 = (bf16[512,256]{1,0:T(8,128)(2,1)}, bf16[512,256]{1,0:T(8,128)(2,1)}, u32[]{:S(2)}, u32[]{:S(2)}) collective-permute-start(bf16[512,256]{1,0:T(8,128)(2,1)} %block_sum.14), channel_id=1, source_target_pairs={{0,16},{4,12},{8,24},{12,4},{16,0},{20,28},{24,8},{28,20},{1,17},{... | collective-permute-start | bytes 786440 | tf_op jit(solution)/shard_map/ppermute | solution.py:691
  390.7 1.2 copy-start.14
  393.9 3.9 collective-permute-start.15
  397.8 0.7 copy-start.15
  401.5 0.9 copy-start.13
  406.5 1.0 copy-start.10
  412.1 1.0 copy-start.11
Sparse Core Ops, SparseCore 0:
  53.7 87.7 all-gather.1
  183.5 76.9 reduce-scatter.2
  262.7 79.3 reduce-scatter.4
